TPU v7x, 256 devices: a whole 4x4x8 slice. The times are simulated.
256 devices in a mesh: shard: 16 (over z, core), model: 4 (over y), unit: 4 (over x).
Axes of the slice: x: 4, y: 4, z: 8, core: 2. Of those that a mesh axis runs over, the one named last changes fastest.
Arguments:
- train_query: bfloat16 [16384, 4096], P(('unit', 'shard'), 'model'), parts along dimension 0, may hold values from -0.125 to 0.125
- low_query: bfloat16 [16384, 16], P(('unit', 'shard')), parts along dimension 0, may hold values from -0.09375 to 0.09375
- high_query: bfloat16 [64, 4096], P('unit', 'model'), parts along dimension 0, may hold values from -1.5 to 1.5
- train_key: bfloat16 [16384, 1024], P(('unit', 'shard'), 'model'), parts along dimension 0, may hold values from -0.125 to 0.125
- low_key: bfloat16 [16384, 16], P(('unit', 'shard')), parts along dimension 0, may hold values from -0.09375 to 0.09375
- high_key: bfloat16 [64, 1024], P('unit', 'model'), parts along dimension 0, may hold values from -1.5 to 1.5
- train_value: bfloat16 [16384, 1024], P(('unit', 'shard'), 'model'), parts along dimension 0, may hold values from -0.125 to 0.125
- low_value: bfloat16 [16384, 16], P(('unit', 'shard')), parts along dimension 0, may hold values from -0.09375 to 0.09375
- high_value: bfloat16 [64, 1024], P('unit', 'model'), parts along dimension 0, may hold values from -1.5 to 1.5
- norm_train: float32 [16384], P(('unit', 'shard', 'model')), parts along dimension 0, may hold values from 0.25 to 1.75
- norm_step: float32 [16384], P(('unit', 'shard', 'model')), parts along dimension 0, may hold values from -0.3 to 0.3
Outputs:
- serving_query: bfloat16 [16384, 4096], P('unit', 'model'), parts along dimension 0
- serving_key: bfloat16 [16384, 1024], P('unit', 'model'), parts along dimension 0
- serving_value: bfloat16 [16384, 1024], P('unit', 'model'), parts along dimension 0
- scale_query: float32 [16384], P(('unit', 'model')), parts along dimension 0
- scale_key: float32 [4096], P(('unit', 'model')), parts along dimension 0
- scale_value: float32 [4096], P(('unit', 'model')), parts along dimension 0
- serve_norm: bfloat16 [16384], P('unit'), parts along dimension 0
There are 4 independent parts, one for each index of `unit`. A program takes and returns all parts, laid end to end along the dimension named above; each array names one. Nothing has to cross between parts.
All inputs are finite; a program needn't handle non-finite values. Where the computation divides by a largest or mean magnitude, that divisor is 1e-20 or more.
Results may differ from a plain program's by a relative error of at most 0.001.
Values may be sent and summed in bfloat16 or wider, within the bound.
A program may use at most 64 MiB of HBM per device.

v0:
```python
import jax
import jax.numpy as jnp
from jax import lax
from jax.sharding import PartitionSpec as P

mix_rate = 1.0


def copy_for_each(x, axis):
    count = lax.axis_size(axis)
    return lax.all_to_all(jnp.broadcast_to(x[None], (count, *x.shape)), axis, 0, 0, tiled=True)


def of_everyone(x, axis):
    everything = copy_for_each(x, axis)
    return jnp.max(everything, axis=0)


def in_one(arrays, axis):
    ends = [0]
    for a in arrays:
        ends.append(ends[-1] + a.size)
    subtotal = of_everyone(jnp.concatenate([a.ravel() for a in arrays]), axis)
    return tuple((subtotal[b:e].reshape(a.shape) for a, b, e in zip(arrays, ends, ends[1:])))


def in_one_piece(arrays, axis, dim, along):
    ends, at = ([], 0)
    for a in arrays[:-1]:
        at += a.shape[along]
        ends.append(at)
    both = jnp.concatenate(arrays, axis=along)
    return tuple(jnp.split(lax.all_gather(both, axis, axis=dim, tiled=True), ends, axis=along))


def laid_out(parts, dim):
    parts = jnp.moveaxis(parts, 0, dim)
    lengths = parts.shape
    return parts.reshape(*lengths[:dim], lengths[dim] * lengths[dim + 1], *lengths[dim + 2 :])


def gathered_copies(x, axis, dim):
    parts = copy_for_each(x, axis)
    return laid_out(parts, dim)


def local(
    train_query,
    low_query,
    high_query,
    train_key,
    low_key,
    high_key,
    train_value,
    low_value,
    high_value,
    norm_train,
    norm_step,
):
    whole_query = train_query.astype(jnp.float32) + mix_rate * jnp.dot(
        low_query, high_query, preferred_element_type=jnp.float32
    )
    whole_key = train_key.astype(jnp.float32) + mix_rate * jnp.dot(
        low_key, high_key, preferred_element_type=jnp.float32
    )
    whole_value = train_value.astype(jnp.float32) + mix_rate * jnp.dot(
        low_value, high_value, preferred_element_type=jnp.float32
    )
    scale_query, scale_key, scale_value = in_one(
        (
            jnp.max(jnp.abs(whole_query), axis=0),
            jnp.max(jnp.abs(whole_key), axis=0),
            jnp.max(jnp.abs(whole_value), axis=0),
        ),
        "shard",
    )
    narrow_query, narrow_key, narrow_value = (
        (whole_query / scale_query).astype(jnp.bfloat16),
        (whole_key / scale_key).astype(jnp.bfloat16),
        (whole_value / scale_value).astype(jnp.bfloat16),
    )
    serving_query, serving_key, serving_value = in_one_piece(
        (narrow_query, narrow_key, narrow_value), "shard", 0, 1
    )
    serve_norm = gathered_copies(
        (norm_train + norm_step).astype(jnp.bfloat16), ("shard", "model"), 0
    )
    return (
        serving_query,
        serving_key,
        serving_value,
        scale_query,
        scale_key,
        scale_value,
        serve_norm,
    )


def solution(mesh):
    in_specs = (
        P(("unit", "shard"), "model"),
        P(("unit", "shard"), None),
        P("unit", "model"),
        P(("unit", "shard"), "model"),
        P(("unit", "shard"), None),
        P("unit", "model"),
        P(("unit", "shard"), "model"),
        P(("unit", "shard"), None),
        P("unit", "model"),
        P(("unit", "shard", "model")),
        P(("unit", "shard", "model")),
    )
    out_specs = (
        P("unit", "model"),
        P("unit", "model"),
        P("unit", "model"),
        P(("unit", "model")),
        P(("unit", "model")),
        P(("unit", "model")),
        P("unit"),
    )
    return jax.shard_map(local, mesh=mesh, in_specs=in_specs, out_specs=out_specs, check_vma=False)
```

profile of v0, /device:TPU:1, one launch (start us, length us, event | category | flops | bytes accessed | tf_op | source)
XLA Modules:
  0.0 122.9 jit_solution(5789545763744168269)
XLA Ops:
  7.2 0.0 copy-start
  7.2 0.0 copy-start.1
  7.2 0.0 all-gather.2.cloned.1.call-start
  7.2 0.7 copy-done
  7.9 1.4 %abs_reduce_fusion = (f32[1024]{0:T(1024)S(1)}, f32[256,1024]{1,0:T(8,128)S(1)}) fusion(bf16[256,16]{0,1:T(8,128)(2,1)} %param.12, bf16[16,1024]{1,0:T(8,128)(2,1)S(1)} %copy-done, bf16[256,1024]{1,0:T(8,128)(2,1)} %param.11), kind=kOutput, calls=%fused_computation.4 | convolution fusion | flops 9436160 | bytes 1617920 | tf_op jit(solution)/shard_map/dot_general | solution.py:60
  9.3 1.2 abs_reduce_fusion.1
  10.5 0.0 copy-done.1
  10.5 1.0 abs_reduce_fusion.2
  11.5 0.1 broadcast_in_dim.4
  11.5 18.2 %all_to_all.12 = f32[16,1,1536]{2,1,0:T(1,128)S(1)} all-to-all(f32[16,1,1536]{2,1,0:T(1,128)S(1)} %broadcast_in_dim.4), channel_id=1, replica_groups=mesh['shard'=16,'model'=4,'unit'=4] {'shard'}, dimensions={0} | all-to-all | bytes 196608 | tf_op jit(solution)/shard_map/all_to_all | solution.py:11
  29.8 0.1 reduce_max.39
  29.8 0.0 copy-start.3
  29.9 0.0 copy-start.4
  29.9 0.0 copy-start.2
  29.9 0.0 copy-start.5
  29.9 0.0 copy-start.6
  29.9 0.1 divide_convert_fusion
  30.1 0.9 pad_maximum_fusion
  31.0 0.0 all-gather.2.cloned.1.call-update
  31.0 0.0 copy-done.3
  31.0 0.0 copy-done.4
  31.1 0.0 copy-done.2
  31.1 0.0 copy-done.5
  31.1 0.0 copy-done.6
  31.1 14.8 %all_to_all.13 = bf16[64,1,64]{2,1,0:T(2,128)(2,1)S(1)} all-to-all(bf16[64,1,64]{2,1,0:T(2,128)(2,1)S(1)} %broadcast_in_dim.5), channel_id=1, replica_groups=mesh['shard'=16,'model'=4,'unit'=4] {'shard','model'}, dimensions={0} | all-to-all | bytes 16384 | tf_op jit(solution)/shard_map/all_to_all | solution.py:11
  45.9 0.1 reduce.1
  46.0 0.7 reshape.33
  46.7 57.1 %all-gather.2.cloned.1.call-done = bf16[4096,1536]{1,0:T(8,128)(2,1)} async-done(((bf16[256,1536]{1,0:T(8,128)(2,1)}), bf16[4096,1536]{1,0:T(8,128)(2,1)}) %all-gather.2.cloned.1.call-update) | async-done | bytes 12582928 | tf_op jit(solution)/shard_map/all_gather | solution.py:33
  103.7 4.5 %fusion = (bf16[4096,256]{1,0:T(8,128)(2,1)}, bf16[4096,256]{1,0:T(8,128)(2,1)}) fusion(bf16[4096,1536]{1,0:T(8,128)(2,1)} %all-gather.2.cloned.1.call-done), kind=kLoop, calls=%fused_computation.12 | loop fusion | bytes 8388608 | tf_op jit(solution)/shard_map/split | solution.py:33
  108.3 7.8 %split.12 = bf16[4096,1024]{1,0:T(8,128)(2,1)} slice(bf16[4096,1536]{1,0:T(8,128)(2,1)} %all-gather.2.cloned.1.call-done), slice={[0:4096], [0:1024]} | slice | bytes 16777216 | tf_op jit(solution)/shard_map/split | solution.py:33
  (6 shorter events, 0.1 us)
Async XLA Ops:
  7.2 0.8 copy-start
  7.2 3.3 %copy-start.1 = (bf16[256,256]{1,0:T(8,128)(2,1)S(1)}, bf16[256,256]{1,0:T(8,128)(2,1)}, u32[]{:S(2)}) copy-start(bf16[256,256]{1,0:T(8,128)(2,1)} %param.14) | copy-start | bytes 393220
  7.2 96.6 %all-gather.2.cloned.1.call-start = ((), (), s32[]{:S(2)}) async-start(), calls=%async_computation.2 | async-start | bytes 13369344 | tf_op jit(solution)/shard_map/all_gather | solution.py:33
  29.8 1.2 copy-start.3
  29.9 1.2 copy-start.4
  29.9 1.2 copy-start.2
  29.9 1.2 copy-start.5
  29.9 1.2 copy-start.6
Sparse Core Ops, SparseCore 0:
  31.2 72.5 all-gather.1
where the time goes:
time: 123 us
  waiting for transfers between devices  57.1 us (46%)
  blocking collectives  33 us (27%)
  between operations  14.2 us (12%)
  local copies, waits for them, and re-layouts  13.8 us (11%)
  matrix products  3.51 us (3%)
  other arithmetic  1.26 us (1%)
    all_gather x1, waiting for transfers between devices, in_one_piece(): lax.all_gather(both, axis, axis=dim, tiled=True)  57.1 us
    all_to_all x2, blocking collectives, copy_for_each(): lax.all_to_all(jnp.broadcast_to(x[None], (count, *x.shape)), axis, 0, 0,...  33 us
    split x2, local copies, waits for them, and re-layouts, in_one_piece(): jnp.split(lax.all_gather(both, axis, axis=dim, tiled=True), ends, axis=al...  12.3 us
  transfers between devices with their start and end apart: 1, of which 1 were waited for; matrix products, arithmetic and copies ran while one was open for 1% of the time, Pallas kernels for 0%

commit v1 on v0

v1 whole, which is shorter than its diff:
```python
import functools

import jax
import jax.numpy as jnp
from jax import lax
from jax.experimental import pallas as pl
from jax.experimental.pallas import tpu as pltpu
from jax.sharding import PartitionSpec as P

MESH = pl.DeviceIdType.MESH
F32, BF16 = jnp.float32, jnp.bfloat16
STEPS = 4
LOW, NORM = STEPS, STEPS + 1


def gather_kernel(
    count, models,
    q, k, v, low_q, low_k, low_v, high_q, high_k, high_v, norm_a, norm_b,
    whole, most, norms,
    raw, low_t, low_n, high, norm_in, norm_all, peak,
    in_sem, y_send, y_recv, ring_send, ring_recv, pair_send, pair_recv,
):
    me, my = lax.axis_index("shard"), lax.axis_index("model")
    right, left = lax.rem(me + 2, count), lax.rem(me + count - 2, count)
    partner = me + 1 - 2 * lax.rem(me, 2)
    over = partner - me
    rank = low_q.shape[0]
    half = raw.shape[1] // 2
    rows = half // STEPS
    hops = count // 4
    units = 2 * hops - 1
    widths = (q.shape[1], k.shape[1], v.shape[1])
    starts = (0, widths[0], widths[0] + widths[1])
    width = sum(widths)

    fetch = []
    for n, (src, start, wide) in enumerate(zip((q, k, v), starts, widths)):
        fetch.append(pltpu.make_async_copy(src, raw.at[me, :, pl.ds(start, wide)], in_sem.at[n]))
    for n, src in enumerate((low_q, low_k, low_v)):
        for h in range(2):
            fetch.append(
                pltpu.make_async_copy(
                    src.at[:, pl.ds(h * half, half)],
                    low_t.at[me, h, pl.ds(n * rank, rank)],
                    in_sem.at[3 + 2 * n + h],
                )
            )
    for n, (src, start, wide) in enumerate(zip((high_q, high_k, high_v), starts, widths)):
        fetch.append(
            pltpu.make_async_copy(src, high.at[pl.ds(n * rank, rank), pl.ds(start, wide)], in_sem.at[9 + n])
        )
    for n, src in enumerate((norm_a, norm_b)):
        fetch.append(pltpu.make_async_copy(src, norm_in.at[n], in_sem.at[12 + n]))
    for copy in fetch:
        copy.start()

    barrier = pltpu.get_barrier_semaphore()
    for other in (partner, right, left):
        pl.semaphore_signal(barrier, inc=1, device_id={"shard": other}, device_id_type=MESH)
    for step in range(1, models):
        pl.semaphore_signal(
            barrier, inc=1, device_id={"model": lax.rem(my + step, models)}, device_id_type=MESH
        )
    for n in range(3):
        for m in range(3):
            if n != m:
                high[n * rank : (n + 1) * rank, starts[m] : starts[m] + widths[m]] = jnp.zeros(
                    (rank, widths[m]), BF16
                )
    peak[...] = jnp.zeros_like(peak)
    pl.semaphore_wait(barrier, 3 + models - 1)

    def part(p, h, j):
        if isinstance(j, int) and j == LOW:
            return low_t.at[p, h]
        if isinstance(j, int) and j == NORM:
            return norm_all.at[p, pl.ds(h * (models // 2), models // 2)]
        return raw.at[p, pl.ds(pl.multiple_of(h * half + j * rows, rows), rows)]

    def hop(way, u, j, p, h):
        ref = part(p, h, j)
        return pltpu.make_async_remote_copy(
            src_ref=ref, dst_ref=ref,
            send_sem=ring_send.at[way, u, j], recv_sem=ring_recv.at[way, u, j],
            device_id={"shard": (right, left)[way]}, device_id_type=MESH,
        )

    def hand(way, u, j, p, h):
        ref = part(p, h, j)
        return pltpu.make_async_remote_copy(
            src_ref=ref, dst_ref=ref,
            send_sem=pair_send.at[way, u, j], recv_sem=pair_recv.at[way, u, j],
            device_id={"shard": partner}, device_id_type=MESH,
        )

    def halves(way, u):
        h = lax.rem(u, 2)
        return h if way == 0 else 1 - h

    def origin(way, u):
        far = 2 * (u // 2 + 1)
        return lax.rem(me + count - far, count) if way == 0 else lax.rem(me + far, count)

    for copy in fetch[:3]:
        copy.wait()

    def send_own(n, j):
        for way in range(2):
            hop(way, n, j, me, n if way == 0 else 1 - n).start()
        hand(2, n, j, me, n).start()

    send_own(0, 0)
    for copy in fetch[3:]:
        copy.wait()
    norm_all[me, my] = norm_in[0] + norm_in[1]
    for j in range(1, STEPS):
        send_own(0, j)
    send_own(0, LOW)
    across = []
    for step in range(1, models):
        ref = norm_all.at[me, my]
        copy = pltpu.make_async_remote_copy(
            src_ref=ref, dst_ref=ref, send_sem=y_send.at[step], recv_sem=y_recv.at[step],
            device_id={"model": lax.rem(my + step, models)}, device_id_type=MESH,
        )
        copy.start()
        across.append(copy)
    for j in range(STEPS):
        send_own(1, j)
    send_own(1, LOW)

    def unfold(slot, p, h):
        low_n[slot] = jnp.transpose(low_t[p, h].astype(F32), (1, 0)).astype(BF16)

    def merge(slot, p, h, s):
        at = pl.ds(pl.multiple_of(h * half + s * rows, rows), rows)
        low = low_n[slot, pl.ds(pl.multiple_of(s * rows, rows), rows), :]
        block = 512
        for c in range(0, width, block):
            cols = slice(c, c + block)
            new = raw[p, at, cols].astype(F32) + jnp.dot(low, high[:, cols], preferred_element_type=F32)
            whole[p, at, cols] = new
            peak[:, cols] = jnp.maximum(
                peak[:, cols], jnp.max(jnp.abs(new).reshape(rows // 8, 8, block), axis=0)
            )

    def merge_half(p, h):
        unfold(0, p, h)

        @pl.loop(0, STEPS)
        def _(s):
            merge(0, p, h, s)

    for h in range(2):
        merge_half(me, h)
    for step in range(1, models):
        across[step - 1].wait_recv()
    for n in range(2):
        send_own(n, NORM)
    for h in range(2):
        for j in range(STEPS + 2):
            hand(2, h, j, partner, h).wait_recv()
        merge_half(partner, h)

    def from_ring(way, u, j, p, h):
        hop(way, u, j, p, h).wait_recv()

        @pl.when(u < units - 2)
        def _():
            hop(way, u + 2, j, p, h).start()

        hand(way, u, j, p, h).start()

    def from_pair(e):
        u, s = e // STEPS, lax.rem(e, STEPS)
        for way in range(2):
            p, h = origin(way, u) + over, halves(way, u)
            hand(way, u, s, p, h).wait_recv()

            @pl.when(s == 0)
            def _():
                hand(way, u, LOW, p, h).wait_recv()
                unfold(2 + way, p, h)

            @pl.when(s == STEPS - 1)
            def _():
                hand(way, u, NORM, p, h).wait_recv()

            merge(2 + way, p, h, s)

    @pl.loop(0, units * STEPS)
    def _(e):
        u, s = e // STEPS, lax.rem(e, STEPS)
        for way in range(2):
            p, h = origin(way, u), halves(way, u)
            from_ring(way, u, s, p, h)

            @pl.when(s == 0)
            def _():
                from_ring(way, u, LOW, p, h)
                unfold(way, p, h)

            @pl.when(s == STEPS - 1)
            def _():
                from_ring(way, u, NORM, p, h)

        for way in range(2):
            merge(way, origin(way, u), halves(way, u), s)

        @pl.when(e > 0)
        def _():
            from_pair(e - 1)

    from_pair(units * STEPS - 1)

    most[...] = peak[...]
    norms[...] = norm_all[...]

    @pl.loop(0, units)
    def _(u):
        for j in range(STEPS + 2):
            for way in range(2):
                hop(way, u, j, me, 0).wait_send()
                hand(way, u, j, me, 0).wait_send()

    for n in range(2):
        for j in range(STEPS + 2):
            hand(2, n, j, me, n).wait_send()
    for copy in across:
        copy.wait_send()


def serve_kernel(
    whole, most, norms,
    q, k, v, scale_q, scale_k, scale_v, norm,
    q_out, k_out, v_out, scale_out, norm_f, norm_out,
    big_sem, sem,
):
    pieces, deep, width = whole.shape
    outs, stages = (q, k, v), (q_out, k_out, v_out)
    widths = tuple(a.shape[1] for a in outs)
    starts = (0, widths[0], widths[0] + widths[1])
    scale_out[...] = jnp.max(most[...], axis=0, keepdims=True)
    small = []
    for n, (dst, start, wide) in enumerate(zip((scale_q, scale_k, scale_v), starts, widths)):
        small.append(pltpu.make_async_copy(scale_out.at[:, pl.ds(start, wide)], dst, sem.at[n]))
    rows = 32

    def out(n, p):
        at = pl.ds(pl.multiple_of(p * deep, deep), deep)
        return pltpu.make_async_copy(stages[n].at[at], outs[n].at[at], big_sem.at[n, p])

    @pl.loop(0, pieces)
    def _(p):
        @pl.loop(0, deep // rows)
        def _(r):
            here = pl.ds(pl.multiple_of(r * rows, rows), rows)
            there = pl.ds(pl.multiple_of(p * deep + r * rows, rows), rows)
            for n in range(3):
                cols = slice(starts[n], starts[n] + widths[n])
                stages[n][there, :] = (whole[p, here, cols] * (1.0 / scale_out[:, cols])).astype(BF16)

        for n in range(3):
            out(n, p).start()

    models = norms.shape[1]
    wide = norms.shape[3]
    for m in range(0, models, 2):
        pair = jnp.concatenate([norms[:, m, 0, :], norms[:, m + 1, 0, :]], axis=1)
        norm_f[pl.ds(m // 2, pieces, stride=models // 2), :] = pair
    norm_out[...] = norm_f[...].astype(BF16)
    small.append(pltpu.make_async_copy(norm_out, norm, sem.at[3]))
    for copy in small:
        copy.start()
    for copy in small:
        copy.wait()

    @pl.loop(0, pieces)
    def _(p):
        for n in range(3):
            out(n, p).wait()


def local(count, models, q, low_q, high_q, k, low_k, high_k, v, low_v, high_v, norm_train, norm_step):
    deep, rank = low_q.shape
    widths = (q.shape[1], k.shape[1], v.shape[1])
    width = sum(widths)
    units = count // 2 - 1
    piece = norm_train.shape[0]
    dma = pltpu.SemaphoreType.DMA
    anywhere = pl.BlockSpec(memory_space=pl.ANY)
    vmem = pl.BlockSpec(memory_space=pltpu.VMEM)
    whole, most, norms = pl.pallas_call(
        functools.partial(gather_kernel, count, models),
        out_shape=(
            pltpu.VMEM((count, deep, width), F32),
            pltpu.VMEM((8, width), F32),
            pltpu.VMEM((count, models, 1, piece), F32),
        ),
        in_specs=[anywhere] * 11,
        out_specs=(vmem, vmem, vmem),
        scratch_shapes=[
            pltpu.VMEM((count, deep, width), BF16),
            pltpu.VMEM((count, 2, 3 * rank, deep // 2), BF16),
            pltpu.VMEM((4, deep // 2, 3 * rank), BF16),
            pltpu.VMEM((3 * rank, width), BF16),
            pltpu.VMEM((2, 1, piece), F32),
            pltpu.VMEM((count, models, 1, piece), F32),
            pltpu.VMEM((8, width), F32),
            dma((14,)),
            dma((models,)),
            dma((models,)),
            dma((2, units, STEPS + 2)),
            dma((2, units, STEPS + 2)),
            dma((3, units, STEPS + 2)),
            dma((3, units, STEPS + 2)),
        ],
        compiler_params=pltpu.CompilerParams(
            collective_id=0, has_side_effects=True, vmem_limit_bytes=20 * 2**20
        ),
        name="gather",
    )(
        *(
            pltpu.with_memory_space_constraint(a, pltpu.HBM)
            for a in (
                q, k, v, low_q.T, low_k.T, low_v.T, high_q, high_k, high_v,
                norm_train.reshape(1, piece), norm_step.reshape(1, piece),
            )
        )
    )
    total = count * deep
    sizes = tuple((total, w) for w in widths)
    serving_q, serving_k, serving_v, scale_q, scale_k, scale_v, norm = pl.pallas_call(
        serve_kernel,
        out_shape=tuple(jax.ShapeDtypeStruct(s, BF16) for s in sizes)
        + tuple(jax.ShapeDtypeStruct((1, w), F32) for w in widths)
        + (jax.ShapeDtypeStruct((count * models // 2, 2 * piece), BF16),),
        in_specs=[vmem] * 3,
        out_specs=(anywhere,) * 7,
        scratch_shapes=[pltpu.VMEM(s, BF16) for s in sizes]
        + [
            pltpu.VMEM((1, width), F32),
            pltpu.VMEM((count * models // 2, 2 * piece), F32),
            pltpu.VMEM((count * models // 2, 2 * piece), BF16),
            dma((3, count)),
            dma((4,)),
        ],
        compiler_params=pltpu.CompilerParams(vmem_limit_bytes=20 * 2**20),
        name="serve",
    )(*(pltpu.with_memory_space_constraint(a, pltpu.VMEM) for a in (whole, most, norms)))
    return (
        serving_q, serving_k, serving_v,
        scale_q.reshape(-1), scale_k.reshape(-1), scale_v.reshape(-1), norm.reshape(-1),
    )


def solution(mesh):
    in_specs = (
        P(("unit", "shard"), "model"),
        P(("unit", "shard"), None),
        P("unit", "model"),
        P(("unit", "shard"), "model"),
        P(("unit", "shard"), None),
        P("unit", "model"),
        P(("unit", "shard"), "model"),
        P(("unit", "shard"), None),
        P("unit", "model"),
        P(("unit", "shard", "model")),
        P(("unit", "shard", "model")),
    )
    out_specs = (
        P("unit", "model"),
        P("unit", "model"),
        P("unit", "model"),
        P(("unit", "model")),
        P(("unit", "model")),
        P(("unit", "model")),
        P("unit"),
    )
    body = functools.partial(local, mesh.shape["shard"], mesh.shape["model"])
    return jax.shard_map(body, mesh=mesh, in_specs=in_specs, out_specs=out_specs, check_vma=False)
```

time: 123 us -> 83.5 us (0.68)
  Pallas kernels: 0 us -> 82.8 us
  waiting for transfers between devices: 57.1 us -> 0 us
  blocking collectives: 33 us -> 0 us
  local copies, waits for them, and re-layouts: 13.8 us -> 0 us
  between operations: 14.2 us -> 0.64 us
  matrix products: 3.51 us -> 0 us
  other arithmetic: 1.26 us -> 0 us
    pallas_call x0 -> x2, Pallas kernels: none -> 82.8 us  [the longest x1 77.5 us: local(): pl.pallas_call(functools.partial(gather_kernel, count, models), out_shape...]
    all_gather x1 -> x0, waiting for transfers between devices: 57.1 us -> none  [in_one_piece(): lax.all_gather(both, axis, axis=dim, tiled=True)]
    all_to_all x2 -> x0, blocking collectives: 33 us -> none  [copy_for_each(): lax.all_to_all(jnp.broadcast_to(x[None], (count, *x.shape)), axis, 0, 0,...]
    split x2 -> x0, local copies, waits for them, and re-layouts: 12.3 us -> none  [in_one_piece(): jnp.split(lax.all_gather(both, axis, axis=dim, tiled=True), ends, axis=al...]
    dot_general x3 -> x0, matrix products: 3.51 us -> none  [the longest x1 1.38 us: local(): jnp.dot(low_query, high_query, preferred_element_type=jnp.float32)]
  transfers between devices with their start and end apart: 1 -> 0, of which waited for: 1 -> 0; matrix products, arithmetic and copies ran while one was open for 1% -> 0% of each run, Pallas kernels for 0% -> 0%
where the time goes in v1:
time: 83.5 us; the launch traced here: 83.4 us
  Pallas kernels  82.8 us (99%)
    pallas_call x1, Pallas kernels, local(): pl.pallas_call(functools.partial(gather_kernel, count, models), out_shape...  77.5 us
    pallas_call x1, Pallas kernels, local(): pl.pallas_call(serve_kernel, out_shape=tuple((jax.ShapeDtypeStruct(s, BF1...  5.26 us

profile of v1, /device:TPU:1, one launch (start us, length us, event | category | flops | bytes accessed | tf_op | source)
XLA Modules:
  0.0 83.4 jit_solution(11553938707706707537)
XLA Ops:
  0.6 77.5 %gather.1 = (f32[16,256,1536]{2,1,0:T(8,128)S(1)}, f32[8,1536]{1,0:T(8,128)S(1)}, f32[16,4,1,64]{3,2,1,0:T(1,128)S(1)}) custom-call(bf16[256,1024]{1,0:T(8,128)(2,1)} %q.1, bf16[256,256]{1,0:T(8,128)(2,1)} %k.1, bf16[256,256]{1,0:T(8,128)(2,1)} %v.1, bf16[16,256]{1,0:T(8,128)(2,1)} %bitcast.9, bf16[16,256]{1,0:T(8,128)(2,1)} %bitcast.10, ...), custom_call_target="tpu_custom_call" | custom-call | tf_op jit(solution)/shard_map/gather/pallas_call | solution.py:293
  78.2 5.3 %serve.1 = (bf16[4096,1024]{1,0:T(8,128)(2,1)}, bf16[4096,256]{1,0:T(8,128)(2,1)}, bf16[4096,256]{1,0:T(8,128)(2,1)}, f32[1,1024]{1,0:T(1,128)}, f32[1,256]{1,0:...) custom-call(f32[16,256,1536]{2,1,0:T(8,128)S(1)} %get-tuple-element.17.whole, f32[8,1536]{1,0:T(8,128)S(1)} %get-tuple-element.18.most, ...), custom_call_target="tpu_custom_call" | custom-call | tf_op jit(solution)/shard_map/serve/pallas_call | solution.py:333

commit v2 on v1

v2 whole, which is shorter than its diff:
```python
import functools

import jax
import jax.numpy as jnp
from jax import lax
from jax.experimental import pallas as pl
from jax.experimental.pallas import tpu as pltpu
from jax.sharding import PartitionSpec as P

MESH = pl.DeviceIdType.MESH
F32, BF16 = jnp.float32, jnp.bfloat16
ROWS = ((0, 64), (64, 32), (96, 16), (112, 16))


def gather_kernel(
    count, models,
    q, k, v, low_q, low_k, low_v, high_q, high_k, high_v, norm_a, norm_b,
    whole, most, norms,
    raw, extra, low_n, high, norm_in, peak,
    in_sem, y_send, y_recv, ring_send, ring_recv, pair_send, pair_recv,
):
    me, my = lax.axis_index("shard"), lax.axis_index("model")
    right, left = lax.rem(me + 2, count), lax.rem(me + count - 2, count)
    partner = me + 1 - 2 * lax.rem(me, 2)
    over = partner - me
    rank = low_q.shape[0]
    half = raw.shape[1] // 2
    hops = count // 4
    full = 2 * (hops - 1)
    widths = (q.shape[1], k.shape[1], v.shape[1])
    starts = (0, widths[0], widths[0] + widths[1])
    width = sum(widths)

    fetch = []
    for n, (src, start, wide) in enumerate(zip((q, k, v), starts, widths)):
        fetch.append(pltpu.make_async_copy(src, raw.at[me, :, pl.ds(start, wide)], in_sem.at[n]))
    at = (
        pl.ds(pl.multiple_of(lax.div(my, 2) * 8, 8), 8),
        pl.ds(pl.multiple_of(lax.rem(my, 2) * half, half), half),
    )
    for n, src in enumerate((low_q, low_k, low_v)):
        fetch.append(pltpu.make_async_copy(src.at[at], extra.at[me, my, n], in_sem.at[3 + n]))
    for n, (src, start, wide) in enumerate(zip((high_q, high_k, high_v), starts, widths)):
        fetch.append(
            pltpu.make_async_copy(src, high.at[pl.ds(n * rank, rank), pl.ds(start, wide)], in_sem.at[6 + n])
        )
    for n, src in enumerate((norm_a, norm_b)):
        fetch.append(pltpu.make_async_copy(src, norm_in.at[n], in_sem.at[9 + n]))
    for copy in fetch[9:] + fetch[:9]:
        copy.start()

    barrier = pltpu.get_barrier_semaphore()
    for other in (partner, right, left):
        pl.semaphore_signal(barrier, inc=1, device_id={"shard": other}, device_id_type=MESH)
    for step in range(1, models):
        pl.semaphore_signal(
            barrier, inc=1, device_id={"model": lax.rem(my + step, models)}, device_id_type=MESH
        )
    for copy in fetch[9:]:
        copy.wait()
    total = norm_in[0] + norm_in[1]
    spread = jnp.concatenate([total, jnp.zeros((1, 128 - total.shape[1]), F32)], axis=1)
    extra[me, my, 3] = jnp.broadcast_to(spread, (8, 128)).astype(BF16)
    for n in range(3):
        for m in range(3):
            if n != m:
                high[n * rank : (n + 1) * rank, starts[m] : starts[m] + widths[m]] = jnp.zeros(
                    (rank, widths[m]), BF16
                )
    peak[...] = jnp.zeros_like(peak)
    for copy in fetch[:9]:
        copy.wait()
    pl.semaphore_wait(barrier, 3 + models - 1)

    def block(p):
        return extra.at[p, my]

    def span(p, h, first=0, rows=half):
        return raw.at[p, pl.ds(pl.multiple_of(h * half + first, 16), rows)]

    def send(ref, sends, recvs, index, to):
        return pltpu.make_async_remote_copy(
            src_ref=ref, dst_ref=ref, send_sem=sends.at[index], recv_sem=recvs.at[index],
            device_id=to, device_id_type=MESH,
        )

    def hop(way, j, ref):
        return send(ref, ring_send, ring_recv, (way, j), {"shard": (right, left)[way]})

    def hand(way, j, ref):
        return send(ref, pair_send, pair_recv, (way, j), {"shard": partner})

    def across(slot, p):
        return [
            send(block(p), y_send, y_recv, (slot, step - 1), {"model": lax.rem(my + step, models)})
            for step in range(1, models)
        ]

    def origin(way, hop_count):
        far = 2 * (hop_count + 1)
        return lax.rem(me + count + (2 * way - 1) * far, count)

    def slot_of(way, kk):
        return 2 + 2 * kk + 2 * hops * way

    def half_of(way, u):
        return lax.rem(u + way, 2)

    HALF, LAST = hops, hops + full

    for way in range(2):
        hop(way, 0, block(me)).start()
        hop(way, HALF, span(me, way)).start()
    hand(2, 0, block(me)).start()
    for copy in across(0, me):
        copy.start()
    hand(2, 1, raw.at[me]).start()
    for way in range(2):
        hop(way, HALF + 1, span(me, 1 - way)).start()

    def unfold(slot, p, h):
        parts = [
            extra[p, quarter + h, n].astype(F32)
            for n in range(3)
            for quarter in range(0, models, 2)
        ]
        low_n[slot] = jnp.transpose(jnp.concatenate(parts, axis=0), (1, 0)).astype(BF16)

    def merge(slot, p, h, first, rows):
        low = low_n[slot, pl.ds(pl.multiple_of(first, 16), rows), :]
        at = pl.ds(pl.multiple_of(h * half + first, 16), rows)
        wide = 512
        for c in range(0, width, wide):
            cols = slice(c, c + wide)
            new = raw[p, at, cols].astype(F32) + jnp.dot(low, high[:, cols], preferred_element_type=F32)
            whole[p, at, cols] = new
            peak[:, cols] = jnp.maximum(
                peak[:, cols], jnp.max(jnp.abs(new).reshape(rows // 8, 8, wide), axis=0)
            )

    def merge_four(which):
        @pl.loop(0, 4)
        def _(j):
            p, h = which(lax.div(j, 2), lax.rem(j, 2))
            unfold(0, p, h)

            @pl.loop(0, half // 32)
            def _(s):
                merge(0, p, h, s * 32, 32)

    def wait_across(slots):
        for slot in slots:
            for copy in across(slot, me):
                copy.wait_recv()

    def merge_event(event):
        if event == 0:
            wait_across((0, 1))
            hand(2, 1, raw.at[partner]).wait_recv()
            merge_four(lambda way, other: (me + other * over, way))
            return
        u = event - 1
        kk = u // 2
        if u % 2 == 0:
            wait_across([slot_of(way, kk) + other for way in range(2) for other in range(2)])
        merge_four(lambda way, other: (origin(way, kk) + other * over, half_of(way, u)))

    def ways(kk):
        return range(2 if kk < hops - 1 else 1)

    def from_pair(event):
        if event == 0:
            hand(2, 0, block(partner)).wait_recv()
            for copy in across(1, partner):
                copy.start()
            return
        u = event - 1
        if event <= hops:
            for way in ways(event - 1):
                p = origin(way, event - 1) + over
                hand(way, event - 1, block(p)).wait_recv()
                for copy in across(slot_of(way, event - 1) + 1, p):
                    copy.start()
        for way in range(2):
            hand(way, HALF + u, span(origin(way, u // 2) + over, half_of(way, u))).wait_recv()

    done = 0
    for event in range(1, full + 1):
        u = event - 1
        kk = u // 2
        for way in range(2):
            p, h = origin(way, kk), half_of(way, u)
            hop(way, HALF + u, span(p, h)).wait_recv()
            if event <= hops and way in ways(event - 1):
                e = origin(way, event - 1)
                hop(way, event - 1, block(e)).wait_recv()
                if way in ways(event) and event < hops:
                    hop(way, event, block(e)).start()
                hand(way, event - 1, block(e)).start()
                for copy in across(slot_of(way, event - 1), e):
                    copy.start()
            if u + 2 < full:
                hop(way, HALF + u + 2, span(p, h)).start()
            elif u + 2 == full:
                for j, (first, rows) in enumerate(ROWS):
                    hop(way, LAST + j, span(p, h, first, rows)).start()
            hand(way, HALF + u, span(p, h)).start()
        from_pair(event - 1)
        if event >= 2:
            merge_event(event - 2)
            done = event - 2
    from_pair(full)
    for event in range(done + 1, full + 1):
        merge_event(event)

    wait_across([slot_of(0, hops - 1) + other for other in range(2)])
    far = origin(0, hops - 1)
    for way in range(2):
        for other in range(2):
            unfold(2 * way + other, far + other * over, way)

    @pl.loop(0, count)
    def _(p):
        norms[p] = extra[p, :, 3]

    def sent(copies):
        for copy in copies:
            copy.wait_send()

    for slot in range(4 * hops):
        sent(across(slot, me))
    sent([hand(2, 0, block(me)), hand(2, 1, raw.at[me])])
    for way in range(2):
        for kk in range(hops):
            if way in ways(kk):
                sent([hop(way, kk, block(me)), hand(way, kk, block(me))])
        for u in range(full):
            sent([hand(way, HALF + u, span(me, 0))])
        for u in range(full - 2):
            sent([hop(way, HALF + u, span(me, 0))])

    def last_pair(j):
        first, rows = ROWS[j]
        for way in range(2):
            hand(way, LAST + j, span(far + over, way, first, rows)).wait_recv()
            merge(2 * way + 1, far + over, way, first, rows)

    for j, (first, rows) in enumerate(ROWS):
        for way in range(2):
            hop(way, LAST + j, span(far, way, first, rows)).wait_recv()
            hand(way, LAST + j, span(far, way, first, rows)).start()
        if j > 0:
            last_pair(j - 1)
        for way in range(2):
            merge(2 * way, far, way, first, rows)
    last_pair(len(ROWS) - 1)
    most[...] = peak[...]

    for way in range(2):
        for u in range(full - 2, full):
            sent([hop(way, HALF + u, span(me, 0))])
        for j, (first, rows) in enumerate(ROWS):
            sent([hop(way, LAST + j, span(me, 0, first, rows)), hand(way, LAST + j, span(me, 0, first, rows))])


def serve_kernel(
    whole, most, norms,
    q, k, v, scale_q, scale_k, scale_v, norm,
    q_out, k_out, v_out, scale_out, per, norm_f, norm_out,
    big_sem, sem,
):
    pieces, deep, width = whole.shape
    outs, stages = (q, k, v), (q_out, k_out, v_out)
    widths = tuple(a.shape[1] for a in outs)
    starts = (0, widths[0], widths[0] + widths[1])
    scale_out[...] = jnp.max(most[...], axis=0, keepdims=True)
    small = []
    for n, (dst, start, wide) in enumerate(zip((scale_q, scale_k, scale_v), starts, widths)):
        small.append(pltpu.make_async_copy(scale_out.at[:, pl.ds(start, wide)], dst, sem.at[n]))
    per[...] = 1.0 / scale_out[...]
    rows = 32

    def out(n, p):
        at = pl.ds(pl.multiple_of(p * deep, deep), deep)
        return pltpu.make_async_copy(stages[n].at[at], outs[n].at[at], big_sem.at[n, p])

    @pl.loop(0, pieces)
    def _(p):
        @pl.loop(0, deep // rows)
        def _(r):
            here = pl.ds(pl.multiple_of(r * rows, rows), rows)
            there = pl.ds(pl.multiple_of(p * deep + r * rows, rows), rows)
            for n in range(3):
                cols = slice(starts[n], starts[n] + widths[n])
                stages[n][there, :] = (whole[p, here, cols] * per[:, cols]).astype(BF16)

        for n in range(3):
            out(n, p).start()

    models = norms.shape[1]
    wide = norm_f.shape[1] // 2
    for m in range(0, models, 2):
        pair = jnp.concatenate(
            [norms[:, n].astype(F32)[:, 0, :wide] for n in (m, m + 1)], axis=1
        )
        norm_f[pl.ds(m // 2, pieces, stride=models // 2), :] = pair
    norm_out[...] = norm_f[...].astype(BF16)
    small.append(pltpu.make_async_copy(norm_out, norm, sem.at[3]))
    for copy in small:
        copy.start()
    for copy in small:
        copy.wait()

    @pl.loop(0, pieces)
    def _(p):
        for n in range(3):
            out(n, p).wait()


def local(count, models, q, low_q, high_q, k, low_k, high_k, v, low_v, high_v, norm_train, norm_step):
    deep, rank = low_q.shape
    widths = (q.shape[1], k.shape[1], v.shape[1])
    width = sum(widths)
    copies = count // 4 + 2 * (count // 4 - 1) + len(ROWS)
    piece = norm_train.shape[0]
    dma = pltpu.SemaphoreType.DMA
    anywhere = pl.BlockSpec(memory_space=pl.ANY)
    vmem = pl.BlockSpec(memory_space=pltpu.VMEM)
    whole, most, norms = pl.pallas_call(
        functools.partial(gather_kernel, count, models),
        out_shape=(
            pltpu.VMEM((count, deep, width), F32),
            pltpu.VMEM((8, width), F32),
            pltpu.VMEM((count, models, 8, 128), BF16),
        ),
        in_specs=[anywhere] * 11,
        out_specs=(vmem, vmem, vmem),
        scratch_shapes=[
            pltpu.VMEM((count, deep, width), BF16),
            pltpu.VMEM((count, models, 4, 8, 128), BF16),
            pltpu.VMEM((4, deep // 2, 3 * rank), BF16),
            pltpu.VMEM((3 * rank, width), BF16),
            pltpu.VMEM((2, 1, piece), F32),
            pltpu.VMEM((8, width), F32),
            dma((11,)),
            dma((count, models - 1)),
            dma((count, models - 1)),
            dma((2, copies)),
            dma((2, copies)),
            dma((3, copies)),
            dma((3, copies)),
        ],
        compiler_params=pltpu.CompilerParams(
            collective_id=0, has_side_effects=True, vmem_limit_bytes=20 * 2**20
        ),
        name="gather",
    )(
        *(
            pltpu.with_memory_space_constraint(a, pltpu.HBM)
            for a in (
                q, k, v, low_q.T, low_k.T, low_v.T, high_q, high_k, high_v,
                norm_train.reshape(1, piece), norm_step.reshape(1, piece),
            )
        )
    )
    total = count * deep
    sizes = tuple((total, w) for w in widths)
    serving_q, serving_k, serving_v, scale_q, scale_k, scale_v, norm = pl.pallas_call(
        serve_kernel,
        out_shape=tuple(jax.ShapeDtypeStruct(s, BF16) for s in sizes)
        + tuple(jax.ShapeDtypeStruct((1, w), F32) for w in widths)
        + (jax.ShapeDtypeStruct((count * models // 2, 2 * piece), BF16),),
        in_specs=[vmem] * 3,
        out_specs=(anywhere,) * 7,
        scratch_shapes=[pltpu.VMEM(s, BF16) for s in sizes]
        + [
            pltpu.VMEM((1, width), F32),
            pltpu.VMEM((1, width), F32),
            pltpu.VMEM((count * models // 2, 2 * piece), F32),
            pltpu.VMEM((count * models // 2, 2 * piece), BF16),
            dma((3, count)),
            dma((4,)),
        ],
        compiler_params=pltpu.CompilerParams(vmem_limit_bytes=20 * 2**20),
        name="serve",
    )(*(pltpu.with_memory_space_constraint(a, pltpu.VMEM) for a in (whole, most, norms)))
    return (
        serving_q, serving_k, serving_v,
        scale_q.reshape(-1), scale_k.reshape(-1), scale_v.reshape(-1), norm.reshape(-1),
    )


def solution(mesh):
    in_specs = (
        P(("unit", "shard"), "model"),
        P(("unit", "shard"), None),
        P("unit", "model"),
        P(("unit", "shard"), "model"),
        P(("unit", "shard"), None),
        P("unit", "model"),
        P(("unit", "shard"), "model"),
        P(("unit", "shard"), None),
        P("unit", "model"),
        P(("unit", "shard", "model")),
        P(("unit", "shard", "model")),
    )
    out_specs = (
        P("unit", "model"),
        P("unit", "model"),
        P("unit", "model"),
        P(("unit", "model")),
        P(("unit", "model")),
        P(("unit", "model")),
        P("unit"),
    )
    body = functools.partial(local, mesh.shape["shard"], mesh.shape["model"])
    return jax.shard_map(body, mesh=mesh, in_specs=in_specs, out_specs=out_specs, check_vma=False)
```

time: 83.5 us -> 83.8 us (level)
  no operation moved by 1% of the time
where the time goes in v2:
time: 83.8 us; the launch traced here: 83.7 us
  Pallas kernels  83.1 us (99%)
    pallas_call x1, Pallas kernels, local(): pl.pallas_call(functools.partial(gather_kernel, count, models), out_shape...  77.9 us
    pallas_call x1, Pallas kernels, local(): pl.pallas_call(serve_kernel, out_shape=tuple((jax.ShapeDtypeStruct(s, BF1...  5.24 us

profile of v2, /device:TPU:1, one launch (start us, length us, event | category | flops | bytes accessed | tf_op | source)
XLA Modules:
  0.0 83.7 jit_solution(11109171206923846497)
XLA Ops:
  0.6 77.9 %gather.1 = (f32[16,256,1536]{2,1,0:T(8,128)S(1)}, f32[8,1536]{1,0:T(8,128)S(1)}, bf16[16,4,8,128]{3,2,1,0:T(8,128)(2,1)S(1)}) custom-call(bf16[256,1024]{1,0:T(8,128)(2,1)} %q.1, bf16[256,256]{1,0:T(8,128)(2,1)} %k.1, bf16[256,256]{1,0:T(8,128)(2,1)} %v.1, bf16[16,256]{1,0:T(8,128)(2,1)} %bitcast.9, bf16[16,256]{1,0:T(8,128)(2,1)} %bitcast.10, ...), custom_call_target="tpu_custom_call" | custom-call | tf_op jit(solution)/shard_map/gather/pallas_call | solution.py:329
  78.5 5.2 %serve.1 = (bf16[4096,1024]{1,0:T(8,128)(2,1)}, bf16[4096,256]{1,0:T(8,128)(2,1)}, bf16[4096,256]{1,0:T(8,128)(2,1)}, f32[1,1024]{1,0:T(1,128)}, f32[1,256]{1,0:...) custom-call(f32[16,256,1536]{2,1,0:T(8,128)S(1)} %get-tuple-element.17.whole, f32[8,1536]{1,0:T(8,128)S(1)} %get-tuple-element.18.most, ...), custom_call_target="tpu_custom_call" | custom-call | tf_op jit(solution)/shard_map/serve/pallas_call | solution.py:368

commit v3 on v2

--- a/solution.py
+++ b/solution.py
@@ -126,13 +126,18 @@
         ]
         low_n[slot] = jnp.transpose(jnp.concatenate(parts, axis=0), (1, 0)).astype(BF16)
 
-    def merge(slot, p, h, first, rows):
+    def merge(slot, p, h, first, rows, ready=False):
         low = low_n[slot, pl.ds(pl.multiple_of(first, 16), rows), :]
         at = pl.ds(pl.multiple_of(h * half + first, 16), rows)
-        wide = 512
+        wide = 256
         for c in range(0, width, wide):
             cols = slice(c, c + wide)
-            new = raw[p, at, cols].astype(F32) + jnp.dot(low, high[:, cols], preferred_element_type=F32)
+            add = (
+                whole[p, at, cols]
+                if ready
+                else jnp.dot(low, high[:, cols], preferred_element_type=F32)
+            )
+            new = raw[p, at, cols].astype(F32) + add
             whole[p, at, cols] = new
             peak[:, cols] = jnp.maximum(
                 peak[:, cols], jnp.max(jnp.abs(new).reshape(rows // 8, 8, wide), axis=0)
@@ -143,10 +148,7 @@
         def _(j):
             p, h = which(lax.div(j, 2), lax.rem(j, 2))
             unfold(0, p, h)
-
-            @pl.loop(0, half // 32)
-            def _(s):
-                merge(0, p, h, s * 32, 32)
+            merge(0, p, h, 0, half)
 
     def wait_across(slots):
         for slot in slots:
@@ -217,7 +219,12 @@
     far = origin(0, hops - 1)
     for way in range(2):
         for other in range(2):
-            unfold(2 * way + other, far + other * over, way)
+            p = far + other * over
+            unfold(2 * way + other, p, way)
+            for c in range(0, width, 256):
+                whole[p, pl.ds(way * half, half), c : c + 256] = jnp.dot(
+                    low_n[2 * way + other], high[:, c : c + 256], preferred_element_type=F32
+                )
 
     @pl.loop(0, count)
     def _(p):
@@ -243,7 +250,7 @@
         first, rows = ROWS[j]
         for way in range(2):
             hand(way, LAST + j, span(far + over, way, first, rows)).wait_recv()
-            merge(2 * way + 1, far + over, way, first, rows)
+            merge(2 * way + 1, far + over, way, first, rows, True)
 
     for j, (first, rows) in enumerate(ROWS):
         for way in range(2):
@@ -252,7 +259,7 @@
         if j > 0:
             last_pair(j - 1)
         for way in range(2):
-            merge(2 * way, far, way, first, rows)
+            merge(2 * way, far, way, first, rows, True)
     last_pair(len(ROWS) - 1)
     most[...] = peak[...]
 

time: 83.8 us -> 79.9 us (0.953)
  Pallas kernels: 83.1 us -> 79.2 us
    pallas_call x1, Pallas kernels: 77.9 us -> 73.9 us  [local(): pl.pallas_call(functools.partial(gather_kernel, count, models), out_shape...]
where the time goes in v3:
time: 79.9 us; the launch traced here: 79.8 us
  Pallas kernels  79.2 us (99%)
    pallas_call x1, Pallas kernels, local(): pl.pallas_call(functools.partial(gather_kernel, count, models), out_shape...  73.9 us
    pallas_call x1, Pallas kernels, local(): pl.pallas_call(serve_kernel, out_shape=tuple((jax.ShapeDtypeStruct(s, BF1...  5.24 us

profile of v3, /device:TPU:1, one launch (start us, length us, event | category | flops | bytes accessed | tf_op | source)
XLA Modules:
  0.0 79.8 jit_solution(16905196586442699467)
XLA Ops:
  0.6 73.9 %gather.1 = (f32[16,256,1536]{2,1,0:T(8,128)S(1)}, f32[8,1536]{1,0:T(8,128)S(1)}, bf16[16,4,8,128]{3,2,1,0:T(8,128)(2,1)S(1)}) custom-call(bf16[256,1024]{1,0:T(8,128)(2,1)} %q.1, bf16[256,256]{1,0:T(8,128)(2,1)} %k.1, bf16[256,256]{1,0:T(8,128)(2,1)} %v.1, bf16[16,256]{1,0:T(8,128)(2,1)} %bitcast.9, bf16[16,256]{1,0:T(8,128)(2,1)} %bitcast.10, ...), custom_call_target="tpu_custom_call" | custom-call | tf_op jit(solution)/shard_map/gather/pallas_call | solution.py:336
  74.6 5.2 %serve.1 = (bf16[4096,1024]{1,0:T(8,128)(2,1)}, bf16[4096,256]{1,0:T(8,128)(2,1)}, bf16[4096,256]{1,0:T(8,128)(2,1)}, f32[1,1024]{1,0:T(1,128)}, f32[1,256]{1,0:...) custom-call(f32[16,256,1536]{2,1,0:T(8,128)S(1)} %get-tuple-element.17.whole, f32[8,1536]{1,0:T(8,128)S(1)} %get-tuple-element.18.most, ...), custom_call_target="tpu_custom_call" | custom-call | tf_op jit(solution)/shard_map/serve/pallas_call | solution.py:375

commit v4 on v3

v4 whole, which is shorter than its diff:
```python
import functools

import jax
import jax.numpy as jnp
from jax import lax
from jax.experimental import pallas as pl
from jax.experimental.pallas import tpu as pltpu
from jax.sharding import PartitionSpec as P

MESH = pl.DeviceIdType.MESH
F32, BF16 = jnp.float32, jnp.bfloat16
ROWS = ((0, 64), (64, 32), (96, 16), (112, 16))


def gather_kernel(
    count, models,
    q, k, v, low_q, low_k, low_v, high_q, high_k, high_v, norm_a, norm_b,
    whole, most, norms,
    raw, extra, mine, low_n, high, norm_in, peak,
    in_sem, y_send, y_recv, e_send, e_recv, give_send, give_recv,
    ring_send, ring_recv, pair_send, pair_recv, ready,
):
    me, my = lax.axis_index("shard"), lax.axis_index("model")
    right, left = lax.rem(me + 2, count), lax.rem(me + count - 2, count)
    core = lax.rem(me, 2)
    first_core = me - core
    partner = me + 1 - 2 * core
    over = partner - me
    lead, rest = core == 0, core == 1
    rank = low_q.shape[0]
    half = raw.shape[1] // 2
    hops = count // 4
    full = 2 * (hops - 1)
    widths = (q.shape[1], k.shape[1], v.shape[1])
    starts = (0, widths[0], widths[0] + widths[1])
    width = sum(widths)

    fetch = []
    for n, (src, start, wide) in enumerate(zip((q, k, v), starts, widths)):
        fetch.append(pltpu.make_async_copy(src, raw.at[me, :, pl.ds(start, wide)], in_sem.at[n]))
    at = (
        pl.ds(pl.multiple_of(lax.div(my, 2) * 8, 8), 8),
        pl.ds(pl.multiple_of(lax.rem(my, 2) * half, half), half),
    )

    def fetch_low(block):
        return [
            pltpu.make_async_copy(src.at[at], block.at[n], in_sem.at[3 + n])
            for n, src in enumerate((low_q, low_k, low_v))
        ]

    for n, (src, start, wide) in enumerate(zip((high_q, high_k, high_v), starts, widths)):
        fetch.append(
            pltpu.make_async_copy(src, high.at[pl.ds(n * rank, rank), pl.ds(start, wide)], in_sem.at[6 + n])
        )
    for n, src in enumerate((norm_a, norm_b)):
        fetch.append(pltpu.make_async_copy(src, norm_in.at[n], in_sem.at[9 + n]))
    for copy in fetch[6:] + fetch[:6]:
        copy.start()

    @pl.when(lead)
    def _():
        for copy in fetch_low(extra.at[my, me]):
            copy.start()

    @pl.when(rest)
    def _():
        for copy in fetch_low(mine):
            copy.start()

    barrier = pltpu.get_barrier_semaphore()

    def tell(other):
        pl.semaphore_signal(barrier, inc=1, device_id=other, device_id_type=MESH)

    for chip in (first_core + 2, first_core + count - 2):
        tell({"shard": lax.rem(chip, count) + 1})

    @pl.when(lead)
    def _():
        tell({"shard": partner})
        for step in range(1, models):
            tell({"model": lax.rem(my + step, models)})

    for copy in fetch[6:]:
        copy.wait()
    total = norm_in[0] + norm_in[1]
    spread = jnp.concatenate([total, jnp.zeros((1, 128 - total.shape[1]), F32)], axis=1)
    tile = jnp.broadcast_to(spread, (8, 128)).astype(BF16)

    @pl.when(lead)
    def _():
        extra[my, me, 3] = tile

    @pl.when(rest)
    def _():
        mine[3] = tile

    for n in range(3):
        for m in range(3):
            if n != m:
                high[n * rank : (n + 1) * rank, starts[m] : starts[m] + widths[m]] = jnp.zeros(
                    (rank, widths[m]), BF16
                )
    peak[...] = jnp.zeros_like(peak)
    for copy in fetch[:6]:
        copy.wait()

    @pl.when(lead)
    def _():
        for copy in fetch_low(extra.at[my, me]):
            copy.wait()

    @pl.when(rest)
    def _():
        for copy in fetch_low(mine):
            copy.wait()

    @pl.when(rest)
    def _():
        pl.semaphore_wait(barrier, 5)
        pl.semaphore_signal(ready, inc=1, device_id={"shard": partner}, device_id_type=MESH)

    @pl.when(lead)
    def _():
        pl.semaphore_wait(ready, 1)

    def block(chip):
        return extra.at[my, pl.ds(chip, 2)]

    def span(p, h, first=0, rows=half):
        return raw.at[p, pl.ds(pl.multiple_of(h * half + first, 16), rows)]

    def send(ref, sends, recvs, index, to):
        return pltpu.make_async_remote_copy(
            src_ref=ref, dst_ref=ref, send_sem=sends.at[index], recv_sem=recvs.at[index],
            device_id=to, device_id_type=MESH,
        )

    def hop(way, j, ref):
        return send(ref, ring_send, ring_recv, (way, j), {"shard": (right, left)[way]})

    def hand(way, j, ref):
        return send(ref, pair_send, pair_recv, (way, j), {"shard": partner})

    def pass_on(way, kk, chip):
        return send(block(chip), e_send, e_recv, (way, kk), {"shard": (right, left)[way]})

    def across(slot, chip):
        return [
            send(block(chip), y_send, y_recv, (slot, step - 1), {"model": lax.rem(my + step, models)})
            for step in range(1, models)
        ]

    def give(slot, chip):
        return send(extra.at[:, pl.ds(chip, 2)], give_send, give_recv, (slot,), {"shard": partner})

    def give_own(p):
        return pltpu.make_async_remote_copy(
            src_ref=mine, dst_ref=extra.at[my, p],
            send_sem=give_send.at[2 * hops], recv_sem=give_recv.at[2 * hops],
            device_id={"shard": partner}, device_id_type=MESH,
        )

    def origin(way, hop_count):
        far = 2 * (hop_count + 1)
        return lax.rem(me + count + (2 * way - 1) * far, count)

    def chip_of(way, hop_count):
        return origin(way, hop_count) - core

    def slot_of(way, kk):
        return 1 + kk + hops * way

    def half_of(way, u):
        return lax.rem(u + way, 2)

    LAST = full

    for way in range(2):
        hop(way, 0, span(me, way)).start()

    @pl.when(rest)
    def _():
        give_own(me).start()

    hand(2, 0, raw.at[me]).start()

    @pl.when(lead)
    def _():
        give_own(partner).wait_recv()
        for way in range(2):
            pass_on(way, 0, first_core).start()

    for way in range(2):
        hop(way, 1, span(me, 1 - way)).start()

    def unfold(slot, p, h):
        parts = [
            extra[quarter + h, p, n].astype(F32)
            for n in range(3)
            for quarter in range(0, models, 2)
        ]
        low_n[slot] = jnp.transpose(jnp.concatenate(parts, axis=0), (1, 0)).astype(BF16)

    def merge(p, h, first, rows, formed=False):
        at = pl.ds(pl.multiple_of(h * half + first, 16), rows)
        wide = 256
        for c in range(0, width, wide):
            cols = slice(c, c + wide)
            add = (
                whole[p, at, cols]
                if formed
                else jnp.dot(low_n[0], high[:, cols], preferred_element_type=F32)
            )
            new = raw[p, at, cols].astype(F32) + add
            whole[p, at, cols] = new
            peak[:, cols] = jnp.maximum(
                peak[:, cols], jnp.max(jnp.abs(new).reshape(rows // 8, 8, wide), axis=0)
            )

    def merge_four(which):
        @pl.loop(0, 4)
        def _(j):
            p, h = which(lax.div(j, 2), lax.rem(j, 2))
            unfold(0, p, h)
            merge(p, h, 0, half)

    def ways(kk):
        return range(2 if kk < hops - 1 else 1)

    def held(kk):
        return [(0, first_core)] * (kk == 0) + [(slot_of(way, kk), chip_of(way, kk)) for way in ways(kk)]

    def collect(kk):
        @pl.when(lead)
        def _():
            for slot, chip in held(kk):
                for copy in across(slot, chip):
                    copy.wait_recv()
                give(slot, chip).start()

    def given(slot, chip):
        @pl.when(rest)
        def _():
            give(slot, chip).wait_recv()

    def merge_event(event):
        if event == 0:
            given(0, first_core)
            hand(2, 0, raw.at[partner]).wait_recv()
            merge_four(lambda way, other: (me + other * over, way))
            return
        u = event - 1
        kk = u // 2
        if u % 2 == 0:
            for way in range(2):
                given(slot_of(way, kk), chip_of(way, kk))
        merge_four(lambda way, other: (origin(way, kk) + other * over, half_of(way, u)))

    def far_products():
        given(slot_of(0, hops - 1), chip_of(0, hops - 1))

        @pl.loop(0, 4)
        def _(j):
            way, other = lax.div(j, 2), lax.rem(j, 2)
            p = far + other * over
            unfold(0, p, way)
            at = pl.ds(pl.multiple_of(way * half, half), half)
            for c in range(0, width, 256):
                whole[p, at, c : c + 256] = jnp.dot(low_n[0], high[:, c : c + 256], preferred_element_type=F32)

    far = origin(0, hops - 1)
    todo = list(range(full + 1))
    for event in range(1, full + 1):
        u = event - 1
        kk = u // 2
        for way in range(2):
            p, h = origin(way, kk), half_of(way, u)
            hop(way, u, span(p, h)).wait_recv()
            if u + 2 < full:
                hop(way, u + 2, span(p, h)).start()
            elif u + 2 == full:
                for j, (first, rows) in enumerate(ROWS):
                    hop(way, LAST + j, span(p, h, first, rows)).start()
            hand(way, u, span(p, h)).start()
        if event <= hops:

            @pl.when(lead)
            def _():
                for way in ways(event - 1):
                    chip = chip_of(way, event - 1)
                    pass_on(way, event - 1, chip).wait_recv()
                    if event < hops and way in ways(event):
                        pass_on(way, event, chip).start()
                if event == 1:
                    pl.semaphore_wait(barrier, models - 1)
                for slot, chip in held(event - 1):
                    for copy in across(slot, chip):
                        copy.start()

        if 2 <= event <= hops + 1:
            collect(event - 2)
        if event >= 2:
            for way in range(2):
                hand(way, u - 1, span(origin(way, (u - 1) // 2) + over, half_of(way, u - 1))).wait_recv()
        while todo and todo[0] + (2 if event >= full - 1 else 3) <= event:
            merge_event(todo.pop(0))
        if event == full:
            if full < hops + 1:
                collect(hops - 1)
            far_products()
    for way in range(2):
        hand(way, full - 1, span(origin(way, (full - 1) // 2) + over, half_of(way, full - 1))).wait_recv()
    for event in todo:
        merge_event(event)

    @pl.loop(0, count)
    def _(p):
        norms[:, p] = extra[:, p, 3]

    def sent(copies):
        for copy in copies:
            copy.wait_send()

    @pl.when(lead)
    def _():
        for slot in range(2 * hops):
            sent(across(slot, first_core) + [give(slot, first_core)])
        for kk in range(hops):
            sent([pass_on(way, kk, first_core) for way in ways(kk)])

    @pl.when(rest)
    def _():
        sent([give_own(me)])

    sent([hand(2, 0, raw.at[me])])
    for way in range(2):
        sent([hand(way, u, span(me, 0)) for u in range(full)])
        sent([hop(way, u, span(me, 0)) for u in range(full - 2)])

    def last_pair(j):
        first, rows = ROWS[j]
        for way in range(2):
            hand(way, LAST + j, span(far + over, way, first, rows)).wait_recv()
            merge(far + over, way, first, rows, True)

    for j, (first, rows) in enumerate(ROWS):
        for way in range(2):
            hop(way, LAST + j, span(far, way, first, rows)).wait_recv()
            hand(way, LAST + j, span(far, way, first, rows)).start()
        if j > 0:
            last_pair(j - 1)
        for way in range(2):
            merge(far, way, first, rows, True)
    last_pair(len(ROWS) - 1)
    most[...] = peak[...]

    for way in range(2):
        for u in range(full - 2, full):
            sent([hop(way, u, span(me, 0))])
        for j, (first, rows) in enumerate(ROWS):
            sent([hop(way, LAST + j, span(me, 0, first, rows)), hand(way, LAST + j, span(me, 0, first, rows))])


def serve_kernel(
    whole, most, norms,
    q, k, v, scale_q, scale_k, scale_v, norm,
    q_out, k_out, v_out, scale_out, per, norm_f, norm_out,
    big_sem, sem,
):
    pieces, deep, width = whole.shape
    outs, stages = (q, k, v), (q_out, k_out, v_out)
    widths = tuple(a.shape[1] for a in outs)
    starts = (0, widths[0], widths[0] + widths[1])
    scale_out[...] = jnp.max(most[...], axis=0, keepdims=True)
    small = []
    for n, (dst, start, wide) in enumerate(zip((scale_q, scale_k, scale_v), starts, widths)):
        small.append(pltpu.make_async_copy(scale_out.at[:, pl.ds(start, wide)], dst, sem.at[n]))
    per[...] = 1.0 / scale_out[...]
    rows = 32

    def out(n, p):
        at = pl.ds(pl.multiple_of(p * deep, deep), deep)
        return pltpu.make_async_copy(stages[n].at[at], outs[n].at[at], big_sem.at[n, p])

    @pl.loop(0, pieces)
    def _(p):
        @pl.loop(0, deep // rows)
        def _(r):
            here = pl.ds(pl.multiple_of(r * rows, rows), rows)
            there = pl.ds(pl.multiple_of(p * deep + r * rows, rows), rows)
            for n in range(3):
                cols = slice(starts[n], starts[n] + widths[n])
                stages[n][there, :] = (whole[p, here, cols] * per[:, cols]).astype(BF16)

        for n in range(3):
            out(n, p).start()

    models = norms.shape[0]
    wide = norm_f.shape[1] // 2
    for m in range(0, models, 2):
        pair = jnp.concatenate(
            [norms[n].astype(F32)[:, 0, :wide] for n in (m, m + 1)], axis=1
        )
        norm_f[pl.ds(m // 2, pieces, stride=models // 2), :] = pair
    norm_out[...] = norm_f[...].astype(BF16)
    small.append(pltpu.make_async_copy(norm_out, norm, sem.at[3]))
    for copy in small:
        copy.start()
    for copy in small:
        copy.wait()

    @pl.loop(0, pieces)
    def _(p):
        for n in range(3):
            out(n, p).wait()


def local(count, models, q, low_q, high_q, k, low_k, high_k, v, low_v, high_v, norm_train, norm_step):
    deep, rank = low_q.shape
    widths = (q.shape[1], k.shape[1], v.shape[1])
    width = sum(widths)
    copies = 2 * (count // 4 - 1) + len(ROWS)
    piece = norm_train.shape[0]
    dma = pltpu.SemaphoreType.DMA
    anywhere = pl.BlockSpec(memory_space=pl.ANY)
    vmem = pl.BlockSpec(memory_space=pltpu.VMEM)
    whole, most, norms = pl.pallas_call(
        functools.partial(gather_kernel, count, models),
        out_shape=(
            pltpu.VMEM((count, deep, width), F32),
            pltpu.VMEM((8, width), F32),
            pltpu.VMEM((models, count, 8, 128), BF16),
        ),
        in_specs=[anywhere] * 11,
        out_specs=(vmem, vmem, vmem),
        scratch_shapes=[
            pltpu.VMEM((count, deep, width), BF16),
            pltpu.VMEM((models, count, 4, 8, 128), BF16),
            pltpu.VMEM((4, 8, 128), BF16),
            pltpu.VMEM((1, deep // 2, 3 * rank), BF16),
            pltpu.VMEM((3 * rank, width), BF16),
            pltpu.VMEM((2, 1, piece), F32),
            pltpu.VMEM((8, width), F32),
            dma((11,)),
            dma((count // 2, models - 1)),
            dma((count // 2, models - 1)),
            dma((2, count // 4)),
            dma((2, count // 4)),
            dma((count // 2 + 1,)),
            dma((count // 2 + 1,)),
            dma((2, copies)),
            dma((2, copies)),
            dma((3, copies)),
            dma((3, copies)),
            pltpu.SemaphoreType.REGULAR,
        ],
        compiler_params=pltpu.CompilerParams(
            collective_id=0, has_side_effects=True, vmem_limit_bytes=20 * 2**20
        ),
        name="gather",
    )(
        *(
            pltpu.with_memory_space_constraint(a, pltpu.HBM)
            for a in (
                q, k, v, low_q.T, low_k.T, low_v.T, high_q, high_k, high_v,
                norm_train.reshape(1, piece), norm_step.reshape(1, piece),
            )
        )
    )
    total = count * deep
    sizes = tuple((total, w) for w in widths)
    serving_q, serving_k, serving_v, scale_q, scale_k, scale_v, norm = pl.pallas_call(
        serve_kernel,
        out_shape=tuple(jax.ShapeDtypeStruct(s, BF16) for s in sizes)
        + tuple(jax.ShapeDtypeStruct((1, w), F32) for w in widths)
        + (jax.ShapeDtypeStruct((count * models // 2, 2 * piece), BF16),),
        in_specs=[vmem] * 3,
        out_specs=(anywhere,) * 7,
        scratch_shapes=[pltpu.VMEM(s, BF16) for s in sizes]
        + [
            pltpu.VMEM((1, width), F32),
            pltpu.VMEM((1, width), F32),
            pltpu.VMEM((count * models // 2, 2 * piece), F32),
            pltpu.VMEM((count * models // 2, 2 * piece), BF16),
            dma((3, count)),
            dma((4,)),
        ],
        compiler_params=pltpu.CompilerParams(vmem_limit_bytes=20 * 2**20),
        name="serve",
    )(*(pltpu.with_memory_space_constraint(a, pltpu.VMEM) for a in (whole, most, norms)))
    return (
        serving_q, serving_k, serving_v,
        scale_q.reshape(-1), scale_k.reshape(-1), scale_v.reshape(-1), norm.reshape(-1),
    )


def solution(mesh):
    in_specs = (
        P(("unit", "shard"), "model"),
        P(("unit", "shard"), None),
        P("unit", "model"),
        P(("unit", "shard"), "model"),
        P(("unit", "shard"), None),
        P("unit", "model"),
        P(("unit", "shard"), "model"),
        P(("unit", "shard"), None),
        P("unit", "model"),
        P(("unit", "shard", "model")),
        P(("unit", "shard", "model")),
    )
    out_specs = (
        P("unit", "model"),
        P("unit", "model"),
        P("unit", "model"),
        P(("unit", "model")),
        P(("unit", "model")),
        P(("unit", "model")),
        P("unit"),
    )
    body = functools.partial(local, mesh.shape["shard"], mesh.shape["model"])
    return jax.shard_map(body, mesh=mesh, in_specs=in_specs, out_specs=out_specs, check_vma=False)
```

time: 79.9 us -> 77.8 us (0.974)
  Pallas kernels: 79.2 us -> 77 us
    pallas_call x1, Pallas kernels: 73.9 us -> 71.8 us  [local(): pl.pallas_call(functools.partial(gather_kernel, count, models), out_shape...]
where the time goes in v4:
time: 77.8 us; the launch traced here: 77.7 us
  Pallas kernels  77 us (99%)
    pallas_call x1, Pallas kernels, local(): pl.pallas_call(functools.partial(gather_kernel, count, models), out_shape...  71.8 us
    pallas_call x1, Pallas kernels, local(): pl.pallas_call(serve_kernel, out_shape=tuple((jax.ShapeDtypeStruct(s, BF1...  5.24 us

profile of v4, /device:TPU:1, one launch (start us, length us, event | category | flops | bytes accessed | tf_op | source)
XLA Modules:
  0.0 77.7 jit_solution(10770928912294132871)
XLA Ops:
  0.6 71.8 %gather.1 = (f32[16,256,1536]{2,1,0:T(8,128)S(1)}, f32[8,1536]{1,0:T(8,128)S(1)}, bf16[4,16,8,128]{3,2,1,0:T(8,128)(2,1)S(1)}) custom-call(bf16[256,1024]{1,0:T(8,128)(2,1)} %q.1, bf16[256,256]{1,0:T(8,128)(2,1)} %k.1, bf16[256,256]{1,0:T(8,128)(2,1)} %v.1, bf16[16,256]{1,0:T(8,128)(2,1)} %bitcast.9, bf16[16,256]{1,0:T(8,128)(2,1)} %bitcast.10, ...), custom_call_target="tpu_custom_call" | custom-call | tf_op jit(solution)/shard_map/gather/pallas_call | solution.py:429
  72.4 5.2 %serve.1 = (bf16[4096,1024]{1,0:T(8,128)(2,1)}, bf16[4096,256]{1,0:T(8,128)(2,1)}, bf16[4096,256]{1,0:T(8,128)(2,1)}, f32[1,1024]{1,0:T(1,128)}, f32[1,256]{1,0:...) custom-call(f32[16,256,1536]{2,1,0:T(8,128)S(1)} %get-tuple-element.17.whole, f32[8,1536]{1,0:T(8,128)S(1)} %get-tuple-element.18.most, ...), custom_call_target="tpu_custom_call" | custom-call | tf_op jit(solution)/shard_map/serve/pallas_call | solution.py:474

commit v5 on v4

--- a/solution.py
+++ b/solution.py
@@ -10,6 +10,8 @@
 MESH = pl.DeviceIdType.MESH
 F32, BF16 = jnp.float32, jnp.bfloat16
 ROWS = ((0, 64), (64, 32), (96, 16), (112, 16))
+MOVED = 2
+BLOCKS = (1, 1, 2, 4, 4, 4)
 
 
 def gather_kernel(
@@ -73,8 +75,14 @@
     def tell(other):
         pl.semaphore_signal(barrier, inc=1, device_id=other, device_id_type=MESH)
 
-    for chip in (first_core + 2, first_core + count - 2):
-        tell({"shard": lax.rem(chip, count) + 1})
+    @pl.when(first_core != count - 2)
+    def _():
+        tell({"shard": lax.rem(first_core + 2, count) + 1})
+
+    @pl.when(first_core == 0)
+    def _():
+        tell({"shard": count - 1})
+
 
     @pl.when(lead)
     def _():
@@ -116,14 +124,33 @@
         for copy in fetch_low(mine):
             copy.wait()
 
-    @pl.when(rest)
+    def say(which, other):
+        pl.semaphore_signal(ready.at[which], inc=1, device_id={"shard": other}, device_id_type=MESH)
+
+    @pl.when(rest & (first_core == 0))
+    def _():
+        pl.semaphore_wait(barrier, 1)
+
+    @pl.when(rest & (first_core != 0) & (first_core != count - 2))
+    def _():
+        pl.semaphore_wait(barrier, 3)
+
+    @pl.when(rest & (first_core == count - 2))
     def _():
         pl.semaphore_wait(barrier, 5)
-        pl.semaphore_signal(ready, inc=1, device_id={"shard": partner}, device_id_type=MESH)
-
-    @pl.when(lead)
-    def _():
-        pl.semaphore_wait(ready, 1)
+        for other in range(2):
+            say(1, other)
+        say(0, partner)
+        pl.semaphore_signal(ready.at[0], inc=1)
+
+    @pl.when(rest & (first_core != 0))
+    def _():
+        for other in range(2):
+            say(0, lax.rem(first_core + count - 2, count) + other)
+        say(1, partner)
+        pl.semaphore_signal(ready.at[1], inc=1)
+
+    pl.semaphore_wait(ready.at[0], 1)
 
     def block(chip):
         return extra.at[my, pl.ds(chip, 2)]
@@ -172,19 +199,27 @@
     def slot_of(way, kk):
         return 1 + kk + hops * way
 
+    def moved(j, ref):
+        return pltpu.make_async_remote_copy(
+            src_ref=ref, dst_ref=ref,
+            send_sem=ring_send.at[1, LAST + len(ROWS) + j - MOVED], recv_sem=ring_recv.at[0, LAST + j],
+            device_id={"shard": left}, device_id_type=MESH,
+        )
+
     def half_of(way, u):
         return lax.rem(u + way, 2)
 
     LAST = full
 
-    for way in range(2):
-        hop(way, 0, span(me, way)).start()
+    hop(0, 0, span(me, 0)).start()
 
     @pl.when(rest)
     def _():
         give_own(me).start()
 
     hand(2, 0, raw.at[me]).start()
+    pl.semaphore_wait(ready.at[1], 1)
+    hop(1, 0, span(me, 1)).start()
 
     @pl.when(lead)
     def _():
@@ -282,7 +317,21 @@
                 hop(way, u + 2, span(p, h)).start()
             elif u + 2 == full:
                 for j, (first, rows) in enumerate(ROWS):
-                    hop(way, LAST + j, span(p, h, first, rows)).start()
+                    if way == 0 and j >= MOVED:
+
+                        @pl.when(first_core != count - 2)
+                        def _():
+                            hop(way, LAST + j, span(p, h, first, rows)).start()
+
+                    else:
+                        hop(way, LAST + j, span(p, h, first, rows)).start()
+            if u + 1 == full and way == 1:
+
+                @pl.when(first_core == 2)
+                def _():
+                    for j in range(MOVED, len(ROWS)):
+                        moved(j, span(p, h, *ROWS[j])).start()
+
             hand(way, u, span(p, h)).start()
         if event <= hops:
 
@@ -304,11 +353,9 @@
         if event >= 2:
             for way in range(2):
                 hand(way, u - 1, span(origin(way, (u - 1) // 2) + over, half_of(way, u - 1))).wait_recv()
-        while todo and todo[0] + (2 if event >= full - 1 else 3) <= event:
+        while todo and todo[0] + (1 if event >= full - 1 else 2) <= event and event >= 3:
             merge_event(todo.pop(0))
-        if event == full:
-            if full < hops + 1:
-                collect(hops - 1)
+        if event == max(full - 1, hops + 1):
             far_products()
     for way in range(2):
         hand(way, full - 1, span(origin(way, (full - 1) // 2) + over, half_of(way, full - 1))).wait_recv()
@@ -360,7 +407,17 @@
         for u in range(full - 2, full):
             sent([hop(way, u, span(me, 0))])
         for j, (first, rows) in enumerate(ROWS):
-            sent([hop(way, LAST + j, span(me, 0, first, rows)), hand(way, LAST + j, span(me, 0, first, rows))])
+            sent([hand(way, LAST + j, span(me, 0, first, rows))])
+            if way == 1 or j < MOVED:
+                sent([hop(way, LAST + j, span(me, 0, first, rows))])
+
+    @pl.when(first_core != count - 2)
+    def _():
+        sent([hop(0, LAST + j, span(me, 0, *ROWS[j])) for j in range(MOVED, len(ROWS))])
+
+    @pl.when(first_core == 2)
+    def _():
+        sent([moved(j, span(me, 0, *ROWS[j])) for j in range(MOVED, len(ROWS))])
 
 
 def serve_kernel(
@@ -380,22 +437,26 @@
     per[...] = 1.0 / scale_out[...]
     rows = 32
 
-    def out(n, p):
-        at = pl.ds(pl.multiple_of(p * deep, deep), deep)
-        return pltpu.make_async_copy(stages[n].at[at], outs[n].at[at], big_sem.at[n, p])
-
-    @pl.loop(0, pieces)
-    def _(p):
-        @pl.loop(0, deep // rows)
-        def _(r):
-            here = pl.ds(pl.multiple_of(r * rows, rows), rows)
-            there = pl.ds(pl.multiple_of(p * deep + r * rows, rows), rows)
-            for n in range(3):
-                cols = slice(starts[n], starts[n] + widths[n])
-                stages[n][there, :] = (whole[p, here, cols] * per[:, cols]).astype(BF16)
+    ends = [sum(BLOCKS[:b]) for b in range(len(BLOCKS) + 1)]
+
+    def out(n, b):
+        at = pl.ds(ends[b] * deep, BLOCKS[b] * deep)
+        return pltpu.make_async_copy(stages[n].at[at], outs[n].at[at], big_sem.at[n, b])
+
+    for b in range(len(BLOCKS)):
+
+        @pl.loop(ends[b], ends[b + 1])
+        def _(p):
+            @pl.loop(0, deep // rows)
+            def _(r):
+                here = pl.ds(pl.multiple_of(r * rows, rows), rows)
+                there = pl.ds(pl.multiple_of(p * deep + r * rows, rows), rows)
+                for n in range(3):
+                    cols = slice(starts[n], starts[n] + widths[n])
+                    stages[n][there, :] = (whole[p, here, cols] * per[:, cols]).astype(BF16)
 
         for n in range(3):
-            out(n, p).start()
+            out(n, b).start()
 
     models = norms.shape[0]
     wide = norm_f.shape[1] // 2
@@ -411,10 +472,9 @@
     for copy in small:
         copy.wait()
 
-    @pl.loop(0, pieces)
-    def _(p):
+    for b in range(len(BLOCKS)):
         for n in range(3):
-            out(n, p).wait()
+            out(n, b).wait()
 
 
 def local(count, models, q, low_q, high_q, k, low_k, high_k, v, low_v, high_v, norm_train, norm_step):
@@ -450,11 +510,11 @@
             dma((2, count // 4)),
             dma((count // 2 + 1,)),
             dma((count // 2 + 1,)),
-            dma((2, copies)),
+            dma((2, copies + len(ROWS) - MOVED)),
             dma((2, copies)),
             dma((3, copies)),
             dma((3, copies)),
-            pltpu.SemaphoreType.REGULAR,
+            pltpu.SemaphoreType.REGULAR((2,)),
         ],
         compiler_params=pltpu.CompilerParams(
             collective_id=0, has_side_effects=True, vmem_limit_bytes=20 * 2**20
@@ -484,7 +544,7 @@
             pltpu.VMEM((1, width), F32),
             pltpu.VMEM((count * models // 2, 2 * piece), F32),
             pltpu.VMEM((count * models // 2, 2 * piece), BF16),
-            dma((3, count)),
+            dma((3, len(BLOCKS))),
             dma((4,)),
         ],
         compiler_params=pltpu.CompilerParams(vmem_limit_bytes=20 * 2**20),

time: 77.8 us -> 76.9 us (0.988)
  Pallas kernels: 77 us -> 76.2 us
where the time goes in v5:
time: 76.9 us; the launch traced here: 76.8 us
  Pallas kernels  76.2 us (99%)
    pallas_call x1, Pallas kernels, local(): pl.pallas_call(functools.partial(gather_kernel, count, models), out_shape...  71.2 us
    pallas_call x1, Pallas kernels, local(): pl.pallas_call(serve_kernel, out_shape=tuple((jax.ShapeDtypeStruct(s, BF1...  4.92 us

profile of v5, /device:TPU:1, one launch (start us, length us, event | category | flops | bytes accessed | tf_op | source)
XLA Modules:
  0.0 76.8 jit_solution(14357003951074896277)
XLA Ops:
  0.6 71.2 %gather.1 = (f32[16,256,1536]{2,1,0:T(8,128)S(1)}, f32[8,1536]{1,0:T(8,128)S(1)}, bf16[4,16,8,128]{3,2,1,0:T(8,128)(2,1)S(1)}) custom-call(bf16[256,1024]{1,0:T(8,128)(2,1)} %q.1, bf16[256,256]{1,0:T(8,128)(2,1)} %k.1, bf16[256,256]{1,0:T(8,128)(2,1)} %v.1, bf16[16,256]{1,0:T(8,128)(2,1)} %bitcast.9, bf16[16,256]{1,0:T(8,128)(2,1)} %bitcast.10, ...), custom_call_target="tpu_custom_call" | custom-call | tf_op jit(solution)/shard_map/gather/pallas_call | solution.py:489
  71.9 4.9 %serve.1 = (bf16[4096,1024]{1,0:T(8,128)(2,1)}, bf16[4096,256]{1,0:T(8,128)(2,1)}, bf16[4096,256]{1,0:T(8,128)(2,1)}, f32[1,1024]{1,0:T(1,128)}, f32[1,256]{1,0:...) custom-call(f32[16,256,1536]{2,1,0:T(8,128)S(1)} %get-tuple-element.17.whole, f32[8,1536]{1,0:T(8,128)S(1)} %get-tuple-element.18.most, ...), custom_call_target="tpu_custom_call" | custom-call | tf_op jit(solution)/shard_map/serve/pallas_call | solution.py:534

commit v6 on v5

--- a/solution.py
+++ b/solution.py
@@ -9,7 +9,7 @@
 
 MESH = pl.DeviceIdType.MESH
 F32, BF16 = jnp.float32, jnp.bfloat16
-ROWS = ((0, 64), (64, 32), (96, 16), (112, 16))
+ROWS = ((0, 128), (128, 64), (192, 32), (224, 32))
 MOVED = 2
 BLOCKS = (1, 1, 2, 4, 4, 4)
 
@@ -32,7 +32,8 @@
     rank = low_q.shape[0]
     half = raw.shape[1] // 2
     hops = count // 4
-    full = 2 * (hops - 1)
+    deep = raw.shape[1]
+    LAST = 3 * (hops - 1)
     widths = (q.shape[1], k.shape[1], v.shape[1])
     starts = (0, widths[0], widths[0] + widths[1])
     width = sum(widths)
@@ -155,8 +156,8 @@
     def block(chip):
         return extra.at[my, pl.ds(chip, 2)]
 
-    def span(p, h, first=0, rows=half):
-        return raw.at[p, pl.ds(pl.multiple_of(h * half + first, 16), rows)]
+    def span(p, first=0, rows=deep):
+        return raw.at[p, pl.ds(first, rows)]
 
     def send(ref, sends, recvs, index, to):
         return pltpu.make_async_remote_copy(
@@ -189,12 +190,9 @@
             device_id={"shard": partner}, device_id_type=MESH,
         )
 
-    def origin(way, hop_count):
-        far = 2 * (hop_count + 1)
-        return lax.rem(me + count + (2 * way - 1) * far, count)
-
-    def chip_of(way, hop_count):
-        return origin(way, hop_count) - core
+    def chip_of(way, kk):
+        far = 2 * (kk + 1)
+        return lax.rem(first_core + count + (2 * way - 1) * far, count)
 
     def slot_of(way, kk):
         return 1 + kk + hops * way
@@ -206,29 +204,44 @@
             device_id={"shard": left}, device_id_type=MESH,
         )
 
-    def half_of(way, u):
-        return lax.rem(u + way, 2)
-
-    LAST = full
-
-    hop(0, 0, span(me, 0)).start()
+    def ways(kk):
+        return range(2 if kk < hops - 1 else 1)
+
+    hand(2, 0, raw.at[me]).start()
 
     @pl.when(rest)
     def _():
+        hop(0, 0, span(me)).start()
         give_own(me).start()
-
-    hand(2, 0, raw.at[me]).start()
-    pl.semaphore_wait(ready.at[1], 1)
-    hop(1, 0, span(me, 1)).start()
+        pl.semaphore_wait(ready.at[1], 1)
+        hop(1, 0, span(me, 0, half)).start()
+        hand(2, 0, raw.at[partner]).wait_recv()
+        for way in range(2):
+            hop(way, 1, span(partner)).start()
+        hop(1, 2, span(me, half, half)).start()
 
     @pl.when(lead)
     def _():
         give_own(partner).wait_recv()
-        for way in range(2):
-            pass_on(way, 0, first_core).start()
-
-    for way in range(2):
-        hop(way, 1, span(me, 1 - way)).start()
+        pass_on(0, 0, first_core).start()
+        pl.semaphore_wait(ready.at[1], 1)
+        pass_on(1, 0, first_core).start()
+        slots = [(0, first_core)]
+        for kk in range(hops):
+            for way in ways(kk):
+                chip = chip_of(way, kk)
+                pass_on(way, kk, chip).wait_recv()
+                if kk + 1 < hops and way in ways(kk + 1):
+                    pass_on(way, kk + 1, chip).start()
+                slots.append((slot_of(way, kk), chip))
+        pl.semaphore_wait(barrier, models - 1)
+        for slot, chip in slots:
+            for copy in across(slot, chip):
+                copy.start()
+        for slot, chip in slots:
+            for copy in across(slot, chip):
+                copy.wait_recv()
+            give(slot, chip).start()
 
     def unfold(slot, p, h):
         parts = [
@@ -238,8 +251,8 @@
         ]
         low_n[slot] = jnp.transpose(jnp.concatenate(parts, axis=0), (1, 0)).astype(BF16)
 
-    def merge(p, h, first, rows, formed=False):
-        at = pl.ds(pl.multiple_of(h * half + first, 16), rows)
+    def merge(p, first, rows, formed=False):
+        at = pl.ds(pl.multiple_of(first, 16), rows)
         wide = 256
         for c in range(0, width, wide):
             cols = slice(c, c + wide)
@@ -254,113 +267,108 @@
                 peak[:, cols], jnp.max(jnp.abs(new).reshape(rows // 8, 8, wide), axis=0)
             )
 
-    def merge_four(which):
-        @pl.loop(0, 4)
-        def _(j):
-            p, h = which(lax.div(j, 2), lax.rem(j, 2))
+    def merge_some(number, which):
+        @pl.loop(0, number)
+        def _(n):
+            p, h = which(n)
             unfold(0, p, h)
-            merge(p, h, 0, half)
-
-    def ways(kk):
-        return range(2 if kk < hops - 1 else 1)
-
-    def held(kk):
-        return [(0, first_core)] * (kk == 0) + [(slot_of(way, kk), chip_of(way, kk)) for way in ways(kk)]
-
-    def collect(kk):
+            merge(p, h * half, half)
+
+    def given(slots):
+        @pl.when(rest)
+        def _():
+            for slot in slots:
+                give(slot, first_core).wait_recv()
+
+    PARTS = (
+        ((0, 1, 0, deep), (1, 1, 0, half)),
+        ((1, 0, 0, deep),),
+        ((0, 0, 0, deep), (1, 1, half, half)),
+    )
+    INDEX = (((0, 2, 0), (1, 3, 0)), ((1, 3, 1),), ((0, 2, 1), (1, 3, 2)))
+
+    def merge_part(kk, part):
+        chips = chip_of(0, kk), chip_of(1, kk)
+
+        def way_chip(way):
+            return chips[0] + way * (chips[1] - chips[0])
+
+        if part == 0:
+            given([slot_of(way, kk) for way in range(2)])
+            merge_some(3, lambda n: (way_chip(lax.div(n, 2)) + 1, lax.rem(n, 2)))
+        elif part == 1:
+            merge_some(2, lambda n: (chips[1], n))
+        else:
+            merge_some(3, lambda n: (way_chip(lax.div(n, 2)) + lax.div(n, 2), lax.div(n + 1, 2)))
+
+    def merge_own():
+        given([0])
+
         @pl.when(lead)
         def _():
-            for slot, chip in held(kk):
-                for copy in across(slot, chip):
-                    copy.wait_recv()
-                give(slot, chip).start()
-
-    def given(slot, chip):
+            hand(2, 0, raw.at[partner]).wait_recv()
+
+        merge_some(4, lambda n: (first_core + lax.div(n, 2), lax.rem(n, 2)))
+
+    far = chip_of(0, hops - 1)
+
+    def far_products():
+        given([slot_of(0, hops - 1)])
+
+        @pl.loop(0, 4)
+        def _(n):
+            p, h = far + lax.div(n, 2), lax.rem(n, 2)
+            unfold(0, p, h)
+            at = pl.ds(pl.multiple_of(h * half, half), half)
+            for c in range(0, width, 256):
+                whole[p, at, c : c + 256] = jnp.dot(low_n[0], high[:, c : c + 256], preferred_element_type=F32)
+
+    todo = [merge_own]
+    events = [(kk, part) for kk in range(hops - 1) for part in range(3)]
+    for e, (kk, part) in enumerate(events):
+        last = kk == hops - 2
+
         @pl.when(rest)
         def _():
-            give(slot, chip).wait_recv()
-
-    def merge_event(event):
-        if event == 0:
-            given(0, first_core)
-            hand(2, 0, raw.at[partner]).wait_recv()
-            merge_four(lambda way, other: (me + other * over, way))
-            return
-        u = event - 1
-        kk = u // 2
-        if u % 2 == 0:
-            for way in range(2):
-                given(slot_of(way, kk), chip_of(way, kk))
-        merge_four(lambda way, other: (origin(way, kk) + other * over, half_of(way, u)))
-
-    def far_products():
-        given(slot_of(0, hops - 1), chip_of(0, hops - 1))
-
-        @pl.loop(0, 4)
-        def _(j):
-            way, other = lax.div(j, 2), lax.rem(j, 2)
-            p = far + other * over
-            unfold(0, p, way)
-            at = pl.ds(pl.multiple_of(way * half, half), half)
-            for c in range(0, width, 256):
-                whole[p, at, c : c + 256] = jnp.dot(low_n[0], high[:, c : c + 256], preferred_element_type=F32)
-
-    far = origin(0, hops - 1)
-    todo = list(range(full + 1))
-    for event in range(1, full + 1):
-        u = event - 1
-        kk = u // 2
-        for way in range(2):
-            p, h = origin(way, kk), half_of(way, u)
-            hop(way, u, span(p, h)).wait_recv()
-            if u + 2 < full:
-                hop(way, u + 2, span(p, h)).start()
-            elif u + 2 == full:
-                for j, (first, rows) in enumerate(ROWS):
-                    if way == 0 and j >= MOVED:
-
-                        @pl.when(first_core != count - 2)
-                        def _():
-                            hop(way, LAST + j, span(p, h, first, rows)).start()
-
-                    else:
-                        hop(way, LAST + j, span(p, h, first, rows)).start()
-            if u + 1 == full and way == 1:
-
-                @pl.when(first_core == 2)
-                def _():
-                    for j in range(MOVED, len(ROWS)):
-                        moved(j, span(p, h, *ROWS[j])).start()
-
-            hand(way, u, span(p, h)).start()
-        if event <= hops:
-
-            @pl.when(lead)
-            def _():
-                for way in ways(event - 1):
-                    chip = chip_of(way, event - 1)
-                    pass_on(way, event - 1, chip).wait_recv()
-                    if event < hops and way in ways(event):
-                        pass_on(way, event, chip).start()
-                if event == 1:
-                    pl.semaphore_wait(barrier, models - 1)
-                for slot, chip in held(event - 1):
-                    for copy in across(slot, chip):
-                        copy.start()
-
-        if 2 <= event <= hops + 1:
-            collect(event - 2)
-        if event >= 2:
-            for way in range(2):
-                hand(way, u - 1, span(origin(way, (u - 1) // 2) + over, half_of(way, u - 1))).wait_recv()
-        while todo and todo[0] + (1 if event >= full - 1 else 2) <= event and event >= 3:
-            merge_event(todo.pop(0))
-        if event == max(full - 1, hops + 1):
+            for (way, piece, first, rows), (_, per_chip, place) in zip(PARTS[part], INDEX[part]):
+                p, n = chip_of(way, kk) + piece, per_chip * kk + place
+                hop(way, n, span(p, first, rows)).wait_recv()
+                if not last:
+                    hop(way, n + per_chip, span(p, first, rows)).start()
+                elif piece != way:
+                    for j, rows_j in enumerate(ROWS):
+                        if way == 0 and j >= MOVED:
+
+                            @pl.when(first_core != count - 2)
+                            def _():
+                                hop(way, LAST + j, span(p, *rows_j)).start()
+
+                        else:
+                            hop(way, LAST + j, span(p, *rows_j)).start()
+                elif way == 1 and part == 2:
+
+                    @pl.when(first_core == 2)
+                    def _():
+                        for j in range(MOVED, len(ROWS)):
+                            moved(j, span(p, *ROWS[j])).start()
+
+                hand(way, n, span(p, first, rows)).start()
+
+        if e >= 2:
+            todo.pop(0)()
+        if e >= 4 and len(todo) > 1:
+            todo.pop(0)()
+        if e == len(events) - 2:
             far_products()
-    for way in range(2):
-        hand(way, full - 1, span(origin(way, (full - 1) // 2) + over, half_of(way, full - 1))).wait_recv()
-    for event in todo:
-        merge_event(event)
+
+        @pl.when(lead)
+        def _():
+            for (way, piece, first, rows), (_, per_chip, place) in zip(PARTS[part], INDEX[part]):
+                hand(way, per_chip * kk + place, span(chip_of(way, kk) + piece, first, rows)).wait_recv()
+
+        todo.append(functools.partial(merge_part, kk, part))
+    for task in todo:
+        task()
 
     @pl.loop(0, count)
     def _(p):
@@ -380,44 +388,44 @@
     @pl.when(rest)
     def _():
         sent([give_own(me)])
+        for kk, part in events:
+            for (way, piece, first, rows), (_, per_chip, place) in zip(PARTS[part], INDEX[part]):
+                n = per_chip * kk + place
+                sent([hand(way, n, span(me, first, rows)), hop(way, n, span(me, first, rows))])
 
     sent([hand(2, 0, raw.at[me])])
-    for way in range(2):
-        sent([hand(way, u, span(me, 0)) for u in range(full)])
-        sent([hop(way, u, span(me, 0)) for u in range(full - 2)])
-
-    def last_pair(j):
-        first, rows = ROWS[j]
+    for j, (first, rows) in enumerate(ROWS):
+
+        @pl.when(rest)
+        def _():
+            for way in range(2):
+                hop(way, LAST + j, span(far + 1 - way, first, rows)).wait_recv()
+                hand(way, LAST + j, span(far + 1 - way, first, rows)).start()
+
+        @pl.when(lead)
+        def _():
+            for way in range(2):
+                hand(way, LAST + j, span(far + 1 - way, first, rows)).wait_recv()
+
         for way in range(2):
-            hand(way, LAST + j, span(far + over, way, first, rows)).wait_recv()
-            merge(far + over, way, first, rows, True)
-
-    for j, (first, rows) in enumerate(ROWS):
+            merge(far + 1 - way, first, rows, True)
+    most[...] = peak[...]
+
+    @pl.when(rest)
+    def _():
         for way in range(2):
-            hop(way, LAST + j, span(far, way, first, rows)).wait_recv()
-            hand(way, LAST + j, span(far, way, first, rows)).start()
-        if j > 0:
-            last_pair(j - 1)
-        for way in range(2):
-            merge(far, way, first, rows, True)
-    last_pair(len(ROWS) - 1)
-    most[...] = peak[...]
-
-    for way in range(2):
-        for u in range(full - 2, full):
-            sent([hop(way, u, span(me, 0))])
-        for j, (first, rows) in enumerate(ROWS):
-            sent([hand(way, LAST + j, span(me, 0, first, rows))])
-            if way == 1 or j < MOVED:
-                sent([hop(way, LAST + j, span(me, 0, first, rows))])
-
-    @pl.when(first_core != count - 2)
-    def _():
-        sent([hop(0, LAST + j, span(me, 0, *ROWS[j])) for j in range(MOVED, len(ROWS))])
-
-    @pl.when(first_core == 2)
-    def _():
-        sent([moved(j, span(me, 0, *ROWS[j])) for j in range(MOVED, len(ROWS))])
+            for j, (first, rows) in enumerate(ROWS):
+                sent([hand(way, LAST + j, span(me, first, rows))])
+                if way == 1 or j < MOVED:
+                    sent([hop(way, LAST + j, span(me, first, rows))])
+
+    @pl.when(rest & (first_core != count - 2))
+    def _():
+        sent([hop(0, LAST + j, span(me, *ROWS[j])) for j in range(MOVED, len(ROWS))])
+
+    @pl.when(rest & (first_core == 2))
+    def _():
+        sent([moved(j, span(me, *ROWS[j])) for j in range(MOVED, len(ROWS))])
 
 
 def serve_kernel(
@@ -481,7 +489,7 @@
     deep, rank = low_q.shape
     widths = (q.shape[1], k.shape[1], v.shape[1])
     width = sum(widths)
-    copies = 2 * (count // 4 - 1) + len(ROWS)
+    copies = 3 * (count // 4 - 1) + len(ROWS)
     piece = norm_train.shape[0]
     dma = pltpu.SemaphoreType.DMA
     anywhere = pl.BlockSpec(memory_space=pl.ANY)

time: 76.9 us -> 76.7 us (level)
  no operation moved by 1% of the time
where the time goes in v6:
time: 76.7 us; the launch traced here: 76.6 us
  Pallas kernels  76 us (99%)
    pallas_call x1, Pallas kernels, local(): pl.pallas_call(functools.partial(gather_kernel, count, models), out_shape...  71.1 us
    pallas_call x1, Pallas kernels, local(): pl.pallas_call(serve_kernel, out_shape=tuple((jax.ShapeDtypeStruct(s, BF1...  4.92 us

profile of v6, /device:TPU:1, one launch (start us, length us, event | category | flops | bytes accessed | tf_op | source)
XLA Modules:
  0.0 76.6 jit_solution(17036030061262200037)
XLA Ops:
  0.6 71.1 %gather.1 = (f32[16,256,1536]{2,1,0:T(8,128)S(1)}, f32[8,1536]{1,0:T(8,128)S(1)}, bf16[4,16,8,128]{3,2,1,0:T(8,128)(2,1)S(1)}) custom-call(bf16[256,1024]{1,0:T(8,128)(2,1)} %q.1, bf16[256,256]{1,0:T(8,128)(2,1)} %k.1, bf16[256,256]{1,0:T(8,128)(2,1)} %v.1, bf16[16,256]{1,0:T(8,128)(2,1)} %bitcast.9, bf16[16,256]{1,0:T(8,128)(2,1)} %bitcast.10, ...), custom_call_target="tpu_custom_call" | custom-call | tf_op jit(solution)/shard_map/gather/pallas_call | solution.py:497
  71.7 4.9 %serve.1 = (bf16[4096,1024]{1,0:T(8,128)(2,1)}, bf16[4096,256]{1,0:T(8,128)(2,1)}, bf16[4096,256]{1,0:T(8,128)(2,1)}, f32[1,1024]{1,0:T(1,128)}, f32[1,256]{1,0:...) custom-call(f32[16,256,1536]{2,1,0:T(8,128)S(1)} %get-tuple-element.17.whole, f32[8,1536]{1,0:T(8,128)S(1)} %get-tuple-element.18.most, ...), custom_call_target="tpu_custom_call" | custom-call | tf_op jit(solution)/shard_map/serve/pallas_call | solution.py:542

commit v7 on v6

--- a/solution.py
+++ b/solution.py
@@ -10,7 +10,7 @@
 MESH = pl.DeviceIdType.MESH
 F32, BF16 = jnp.float32, jnp.bfloat16
 ROWS = ((0, 128), (128, 64), (192, 32), (224, 32))
-MOVED = 2
+MOVED = 3
 BLOCKS = (1, 1, 2, 4, 4, 4)
 
 
@@ -58,7 +58,7 @@
         )
     for n, src in enumerate((norm_a, norm_b)):
         fetch.append(pltpu.make_async_copy(src, norm_in.at[n], in_sem.at[9 + n]))
-    for copy in fetch[6:] + fetch[:6]:
+    for copy in fetch:
         copy.start()
 
     @pl.when(lead)
@@ -90,6 +90,101 @@
         tell({"shard": partner})
         for step in range(1, models):
             tell({"model": lax.rem(my + step, models)})
+
+    def say(which, other):
+        pl.semaphore_signal(ready.at[which], inc=1, device_id={"shard": other}, device_id_type=MESH)
+
+    @pl.when(rest & (first_core == 0))
+    def _():
+        pl.semaphore_wait(barrier, 1)
+
+    @pl.when(rest & (first_core != 0) & (first_core != count - 2))
+    def _():
+        pl.semaphore_wait(barrier, 3)
+
+    @pl.when(rest & (first_core == count - 2))
+    def _():
+        pl.semaphore_wait(barrier, 5)
+        for other in range(2):
+            say(1, other)
+        say(0, partner)
+        pl.semaphore_signal(ready.at[0], inc=1)
+
+    @pl.when(rest & (first_core != 0))
+    def _():
+        for other in range(2):
+            say(0, lax.rem(first_core + count - 2, count) + other)
+        say(1, partner)
+        pl.semaphore_signal(ready.at[1], inc=1)
+
+    for copy in fetch[:3]:
+        copy.wait()
+    pl.semaphore_wait(ready.at[0], 1)
+
+    def block(chip):
+        return extra.at[my, pl.ds(chip, 2)]
+
+    def span(p, first=0, rows=deep):
+        return raw.at[p, pl.ds(first, rows)]
+
+    def send(ref, sends, recvs, index, to):
+        return pltpu.make_async_remote_copy(
+            src_ref=ref, dst_ref=ref, send_sem=sends.at[index], recv_sem=recvs.at[index],
+            device_id=to, device_id_type=MESH,
+        )
+
+    def hop(way, j, ref):
+        return send(ref, ring_send, ring_recv, (way, j), {"shard": (right, left)[way]})
+
+    def hand(way, j, ref):
+        return send(ref, pair_send, pair_recv, (way, j), {"shard": partner})
+
+    def pass_on(way, kk, chip):
+        return send(block(chip), e_send, e_recv, (way, kk), {"shard": (right, left)[way]})
+
+    def across(slot, chip):
+        return [
+            send(block(chip), y_send, y_recv, (slot, step - 1), {"model": lax.rem(my + step, models)})
+            for step in range(1, models)
+        ]
+
+    def give(slot, chip):
+        return send(extra.at[:, pl.ds(chip, 2)], give_send, give_recv, (slot,), {"shard": partner})
+
+    def give_own(p):
+        return pltpu.make_async_remote_copy(
+            src_ref=mine, dst_ref=extra.at[my, p],
+            send_sem=give_send.at[2 * hops], recv_sem=give_recv.at[2 * hops],
+            device_id={"shard": partner}, device_id_type=MESH,
+        )
+
+    def chip_of(way, kk):
+        far = 2 * (kk + 1)
+        return lax.rem(first_core + count + (2 * way - 1) * far, count)
+
+    def slot_of(way, kk):
+        return 1 + kk + hops * way
+
+    def moved(j, ref):
+        return pltpu.make_async_remote_copy(
+            src_ref=ref, dst_ref=ref,
+            send_sem=ring_send.at[1, LAST + len(ROWS) + j - MOVED], recv_sem=ring_recv.at[0, LAST + j],
+            device_id={"shard": left}, device_id_type=MESH,
+        )
+
+    def ways(kk):
+        return range(2 if kk < hops - 1 else 1)
+
+    @pl.when(rest)
+    def _():
+        hop(0, 0, span(me)).start()
+
+    hand(2, 0, raw.at[me]).start()
+
+    @pl.when(rest & (first_core != 0))
+    def _():
+        pl.semaphore_wait(ready.at[1], 1)
+        hop(1, 0, span(me, 0, half)).start()
 
     for copy in fetch[6:]:
         copy.wait()
@@ -112,7 +207,7 @@
                     (rank, widths[m]), BF16
                 )
     peak[...] = jnp.zeros_like(peak)
-    for copy in fetch[:6]:
+    for copy in fetch[3:6]:
         copy.wait()
 
     @pl.when(lead)
@@ -125,96 +220,17 @@
         for copy in fetch_low(mine):
             copy.wait()
 
-    def say(which, other):
-        pl.semaphore_signal(ready.at[which], inc=1, device_id={"shard": other}, device_id_type=MESH)
+    @pl.when(rest)
+    def _():
+        give_own(me).start()
 
     @pl.when(rest & (first_core == 0))
     def _():
-        pl.semaphore_wait(barrier, 1)
-
-    @pl.when(rest & (first_core != 0) & (first_core != count - 2))
-    def _():
-        pl.semaphore_wait(barrier, 3)
-
-    @pl.when(rest & (first_core == count - 2))
-    def _():
-        pl.semaphore_wait(barrier, 5)
-        for other in range(2):
-            say(1, other)
-        say(0, partner)
-        pl.semaphore_signal(ready.at[0], inc=1)
-
-    @pl.when(rest & (first_core != 0))
-    def _():
-        for other in range(2):
-            say(0, lax.rem(first_core + count - 2, count) + other)
-        say(1, partner)
-        pl.semaphore_signal(ready.at[1], inc=1)
-
-    pl.semaphore_wait(ready.at[0], 1)
-
-    def block(chip):
-        return extra.at[my, pl.ds(chip, 2)]
-
-    def span(p, first=0, rows=deep):
-        return raw.at[p, pl.ds(first, rows)]
-
-    def send(ref, sends, recvs, index, to):
-        return pltpu.make_async_remote_copy(
-            src_ref=ref, dst_ref=ref, send_sem=sends.at[index], recv_sem=recvs.at[index],
-            device_id=to, device_id_type=MESH,
-        )
-
-    def hop(way, j, ref):
-        return send(ref, ring_send, ring_recv, (way, j), {"shard": (right, left)[way]})
-
-    def hand(way, j, ref):
-        return send(ref, pair_send, pair_recv, (way, j), {"shard": partner})
-
-    def pass_on(way, kk, chip):
-        return send(block(chip), e_send, e_recv, (way, kk), {"shard": (right, left)[way]})
-
-    def across(slot, chip):
-        return [
-            send(block(chip), y_send, y_recv, (slot, step - 1), {"model": lax.rem(my + step, models)})
-            for step in range(1, models)
-        ]
-
-    def give(slot, chip):
-        return send(extra.at[:, pl.ds(chip, 2)], give_send, give_recv, (slot,), {"shard": partner})
-
-    def give_own(p):
-        return pltpu.make_async_remote_copy(
-            src_ref=mine, dst_ref=extra.at[my, p],
-            send_sem=give_send.at[2 * hops], recv_sem=give_recv.at[2 * hops],
-            device_id={"shard": partner}, device_id_type=MESH,
-        )
-
-    def chip_of(way, kk):
-        far = 2 * (kk + 1)
-        return lax.rem(first_core + count + (2 * way - 1) * far, count)
-
-    def slot_of(way, kk):
-        return 1 + kk + hops * way
-
-    def moved(j, ref):
-        return pltpu.make_async_remote_copy(
-            src_ref=ref, dst_ref=ref,
-            send_sem=ring_send.at[1, LAST + len(ROWS) + j - MOVED], recv_sem=ring_recv.at[0, LAST + j],
-            device_id={"shard": left}, device_id_type=MESH,
-        )
-
-    def ways(kk):
-        return range(2 if kk < hops - 1 else 1)
-
-    hand(2, 0, raw.at[me]).start()
-
-    @pl.when(rest)
-    def _():
-        hop(0, 0, span(me)).start()
-        give_own(me).start()
         pl.semaphore_wait(ready.at[1], 1)
         hop(1, 0, span(me, 0, half)).start()
+
+    @pl.when(rest)
+    def _():
         hand(2, 0, raw.at[partner]).wait_recv()
         for way in range(2):
             hop(way, 1, span(partner)).start()

time: 76.7 us -> 76.5 us (level)
  no operation moved by 1% of the time
where the time goes in v7:
time: 76.5 us; the launch traced here: 76.4 us
  Pallas kernels  75.8 us (99%)
    pallas_call x1, Pallas kernels, local(): pl.pallas_call(functools.partial(gather_kernel, count, models), out_shape...  70.9 us
    pallas_call x1, Pallas kernels, local(): pl.pallas_call(serve_kernel, out_shape=tuple((jax.ShapeDtypeStruct(s, BF1...  4.92 us

profile of v7, /device:TPU:1, one launch (start us, length us, event | category | flops | bytes accessed | tf_op | source)
XLA Modules:
  0.0 76.4 jit_solution(4070913630618642976)
XLA Ops:
  0.6 70.9 %gather.1 = (f32[16,256,1536]{2,1,0:T(8,128)S(1)}, f32[8,1536]{1,0:T(8,128)S(1)}, bf16[4,16,8,128]{3,2,1,0:T(8,128)(2,1)S(1)}) custom-call(bf16[256,1024]{1,0:T(8,128)(2,1)} %q.1, bf16[256,256]{1,0:T(8,128)(2,1)} %k.1, bf16[256,256]{1,0:T(8,128)(2,1)} %v.1, bf16[16,256]{1,0:T(8,128)(2,1)} %bitcast.9, bf16[16,256]{1,0:T(8,128)(2,1)} %bitcast.10, ...), custom_call_target="tpu_custom_call" | custom-call | tf_op jit(solution)/shard_map/gather/pallas_call | solution.py:513
  71.5 4.9 %serve.1 = (bf16[4096,1024]{1,0:T(8,128)(2,1)}, bf16[4096,256]{1,0:T(8,128)(2,1)}, bf16[4096,256]{1,0:T(8,128)(2,1)}, f32[1,1024]{1,0:T(1,128)}, f32[1,256]{1,0:...) custom-call(f32[16,256,1536]{2,1,0:T(8,128)S(1)} %get-tuple-element.17.whole, f32[8,1536]{1,0:T(8,128)S(1)} %get-tuple-element.18.most, ...), custom_call_target="tpu_custom_call" | custom-call | tf_op jit(solution)/shard_map/serve/pallas_call | solution.py:558

commit v8 on v7

--- a/solution.py
+++ b/solution.py
@@ -9,8 +9,8 @@
 
 MESH = pl.DeviceIdType.MESH
 F32, BF16 = jnp.float32, jnp.bfloat16
-ROWS = ((0, 128), (128, 64), (192, 32), (224, 32))
-MOVED = 3
+ROWS = ((0, 128), (128, 80), (208, 16), (224, 32))
+MOVED = 2
 BLOCKS = (1, 1, 2, 4, 4, 4)
 
 
@@ -38,6 +38,26 @@
     starts = (0, widths[0], widths[0] + widths[1])
     width = sum(widths)
 
+    barrier = pltpu.get_barrier_semaphore()
+
+    def tell(other):
+        pl.semaphore_signal(barrier, inc=1, device_id=other, device_id_type=MESH)
+
+    @pl.when(first_core != count - 2)
+    def _():
+        tell({"shard": lax.rem(first_core + 2, count) + 1})
+
+    @pl.when(first_core == 0)
+    def _():
+        tell({"shard": count - 1})
+
+
+    @pl.when(lead)
+    def _():
+        tell({"shard": partner})
+        for step in range(1, models):
+            tell({"model": lax.rem(my + step, models)})
+
     fetch = []
     for n, (src, start, wide) in enumerate(zip((q, k, v), starts, widths)):
         fetch.append(pltpu.make_async_copy(src, raw.at[me, :, pl.ds(start, wide)], in_sem.at[n]))
@@ -70,26 +90,6 @@
     def _():
         for copy in fetch_low(mine):
             copy.start()
-
-    barrier = pltpu.get_barrier_semaphore()
-
-    def tell(other):
-        pl.semaphore_signal(barrier, inc=1, device_id=other, device_id_type=MESH)
-
-    @pl.when(first_core != count - 2)
-    def _():
-        tell({"shard": lax.rem(first_core + 2, count) + 1})
-
-    @pl.when(first_core == 0)
-    def _():
-        tell({"shard": count - 1})
-
-
-    @pl.when(lead)
-    def _():
-        tell({"shard": partner})
-        for step in range(1, models):
-            tell({"model": lax.rem(my + step, models)})
 
     def say(which, other):
         pl.semaphore_signal(ready.at[which], inc=1, device_id={"shard": other}, device_id_type=MESH)

time: 76.5 us -> 76.5 us (level)
  no operation moved by 1% of the time
where the time goes in v8:
time: 76.5 us; the launch traced here: 76.4 us
  Pallas kernels  75.8 us (99%)
    pallas_call x1, Pallas kernels, local(): pl.pallas_call(functools.partial(gather_kernel, count, models), out_shape...  70.9 us
    pallas_call x1, Pallas kernels, local(): pl.pallas_call(serve_kernel, out_shape=tuple((jax.ShapeDtypeStruct(s, BF1...  4.92 us

profile of v8, /device:TPU:1, one launch (start us, length us, event | category | flops | bytes accessed | tf_op | source)
XLA Modules:
  0.0 76.4 jit_solution(17949243463321380756)
XLA Ops:
  0.6 70.9 %gather.1 = (f32[16,256,1536]{2,1,0:T(8,128)S(1)}, f32[8,1536]{1,0:T(8,128)S(1)}, bf16[4,16,8,128]{3,2,1,0:T(8,128)(2,1)S(1)}) custom-call(bf16[256,1024]{1,0:T(8,128)(2,1)} %q.1, bf16[256,256]{1,0:T(8,128)(2,1)} %k.1, bf16[256,256]{1,0:T(8,128)(2,1)} %v.1, bf16[16,256]{1,0:T(8,128)(2,1)} %bitcast.9, bf16[16,256]{1,0:T(8,128)(2,1)} %bitcast.10, ...), custom_call_target="tpu_custom_call" | custom-call | tf_op jit(solution)/shard_map/gather/pallas_call | solution.py:513
  71.5 4.9 %serve.1 = (bf16[4096,1024]{1,0:T(8,128)(2,1)}, bf16[4096,256]{1,0:T(8,128)(2,1)}, bf16[4096,256]{1,0:T(8,128)(2,1)}, f32[1,1024]{1,0:T(1,128)}, f32[1,256]{1,0:...) custom-call(f32[16,256,1536]{2,1,0:T(8,128)S(1)} %get-tuple-element.17.whole, f32[8,1536]{1,0:T(8,128)S(1)} %get-tuple-element.18.most, ...), custom_call_target="tpu_custom_call" | custom-call | tf_op jit(solution)/shard_map/serve/pallas_call | solution.py:558

commit v9 on v8

--- a/solution.py
+++ b/solution.py
@@ -9,9 +9,9 @@
 
 MESH = pl.DeviceIdType.MESH
 F32, BF16 = jnp.float32, jnp.bfloat16
-ROWS = ((0, 128), (128, 80), (208, 16), (224, 32))
+ROWS = ((0, 128), (128, 80), (208, 16), (224, 16), (240, 16))
 MOVED = 2
-BLOCKS = (1, 1, 2, 4, 4, 4)
+BLOCKS = (1, 2, 4, 9)
 
 
 def gather_kernel(

time: 76.5 us -> 77 us (level)
  no operation moved by 1% of the time
where the time goes in v9:
time: 77 us; the launch traced here: 76.9 us
  Pallas kernels  76.2 us (99%)
    pallas_call x1, Pallas kernels, local(): pl.pallas_call(functools.partial(gather_kernel, count, models), out_shape...  71 us
    pallas_call x1, Pallas kernels, local(): pl.pallas_call(serve_kernel, out_shape=tuple((jax.ShapeDtypeStruct(s, BF1...  5.24 us

profile of v9, /device:TPU:1, one launch (start us, length us, event | category | flops | bytes accessed | tf_op | source)
XLA Modules:
  0.0 76.9 jit_solution(17279569518934004105)
XLA Ops:
  0.6 71.0 %gather.1 = (f32[16,256,1536]{2,1,0:T(8,128)S(1)}, f32[8,1536]{1,0:T(8,128)S(1)}, bf16[4,16,8,128]{3,2,1,0:T(8,128)(2,1)S(1)}) custom-call(bf16[256,1024]{1,0:T(8,128)(2,1)} %q.1, bf16[256,256]{1,0:T(8,128)(2,1)} %k.1, bf16[256,256]{1,0:T(8,128)(2,1)} %v.1, bf16[16,256]{1,0:T(8,128)(2,1)} %bitcast.9, bf16[16,256]{1,0:T(8,128)(2,1)} %bitcast.10, ...), custom_call_target="tpu_custom_call" | custom-call | tf_op jit(solution)/shard_map/gather/pallas_call | solution.py:513
  71.6 5.2 %serve.1 = (bf16[4096,1024]{1,0:T(8,128)(2,1)}, bf16[4096,256]{1,0:T(8,128)(2,1)}, bf16[4096,256]{1,0:T(8,128)(2,1)}, f32[1,1024]{1,0:T(1,128)}, f32[1,256]{1,0:...) custom-call(f32[16,256,1536]{2,1,0:T(8,128)S(1)} %get-tuple-element.17.whole, f32[8,1536]{1,0:T(8,128)S(1)} %get-tuple-element.18.most, ...), custom_call_target="tpu_custom_call" | custom-call | tf_op jit(solution)/shard_map/serve/pallas_call | solution.py:558

commit v10 on v8

--- a/solution.py
+++ b/solution.py
@@ -11,7 +11,7 @@
 F32, BF16 = jnp.float32, jnp.bfloat16
 ROWS = ((0, 128), (128, 80), (208, 16), (224, 32))
 MOVED = 2
-BLOCKS = (1, 1, 2, 4, 4, 4)
+BLOCKS = (1, 1, 2, 3, 3, 3, 3)
 
 
 def gather_kernel(

time: 76.5 us -> 76.6 us (level)
  no operation moved by 1% of the time
where the time goes in v10:
time: 76.6 us; the launch traced here: 76.5 us
  Pallas kernels  75.8 us (99%)
    pallas_call x1, Pallas kernels, local(): pl.pallas_call(functools.partial(gather_kernel, count, models), out_shape...  70.9 us
    pallas_call x1, Pallas kernels, local(): pl.pallas_call(serve_kernel, out_shape=tuple((jax.ShapeDtypeStruct(s, BF1...  4.93 us

profile of v10, /device:TPU:1, one launch (start us, length us, event | category | flops | bytes accessed | tf_op | source)
XLA Modules:
  0.0 76.5 jit_solution(9350311140622086446)
XLA Ops:
  0.6 70.9 %gather.1 = (f32[16,256,1536]{2,1,0:T(8,128)S(1)}, f32[8,1536]{1,0:T(8,128)S(1)}, bf16[4,16,8,128]{3,2,1,0:T(8,128)(2,1)S(1)}) custom-call(bf16[256,1024]{1,0:T(8,128)(2,1)} %q.1, bf16[256,256]{1,0:T(8,128)(2,1)} %k.1, bf16[256,256]{1,0:T(8,128)(2,1)} %v.1, bf16[16,256]{1,0:T(8,128)(2,1)} %bitcast.9, bf16[16,256]{1,0:T(8,128)(2,1)} %bitcast.10, ...), custom_call_target="tpu_custom_call" | custom-call | tf_op jit(solution)/shard_map/gather/pallas_call | solution.py:513
  71.5 4.9 %serve.1 = (bf16[4096,1024]{1,0:T(8,128)(2,1)}, bf16[4096,256]{1,0:T(8,128)(2,1)}, bf16[4096,256]{1,0:T(8,128)(2,1)}, f32[1,1024]{1,0:T(1,128)}, f32[1,256]{1,0:...) custom-call(f32[16,256,1536]{2,1,0:T(8,128)S(1)} %get-tuple-element.17.whole, f32[8,1536]{1,0:T(8,128)S(1)} %get-tuple-element.18.most, ...), custom_call_target="tpu_custom_call" | custom-call | tf_op jit(solution)/shard_map/serve/pallas_call | solution.py:558
